TPU v7x, 256 devices: a whole 4x4x8 slice. The times are simulated.
256 devices in a mesh: dom: 256 (over y, x, z, core).
Axes of the slice: x: 4, y: 4, z: 8, core: 2. Of those that a mesh axis runs over, the one named last changes fastest.
Arguments:
- currents: float32 [16, 524288], P(None, 'dom'), may hold values from -36 to 36
- conductance: float32 [524288], P('dom'), may hold values from 0.25 to 4
- ground: float32 [524288], P('dom'), may hold values from 0.1 to 1
- ell_cols: int32 [9, 524288], P(None, 'dom'), may hold values from -1 to 2815, as said below
- send_rows: int32 [1536, 128], P('dom'), may hold values from -1 to 2047, as said below
Outputs:
- voltages: float32 [16, 524288], P(None, 'dom')
- residual: float32 [16, 524288], P(None, 'dom')
Inputs may be any that keep to these rules, and one draw needn't show every extreme that they name: `ell_cols`: column n belongs to the partition of node n. The graph is symmetric: node a names node b in as many slots as b names a, and the two edges of a boundary slot pair the k-th live entries of the rows of partitions p and p + e. Each node has at most one edge to another partition. `send_rows`: row 2 * 3 * p + o lists, for the o-th offset e of -3, ..., -1, 1, ..., 3, the local node numbers of partition p whose values partition p + e reads; live entries come first and the rest are -1. The rows of p toward p + e and of p + e toward p have the same number of live entries, at most 128; in every draw some pair of rows is full. A node appears at most once among its partition's rows. Rows toward partitions outside 0 to 255 are all -1.
All inputs are finite; a program needn't handle non-finite values.
Results may differ from a plain program's by a relative error of at most 0.00011.
Values sent between devices are 32-bit elements; how exact they have to be, the bound alone decides.
A program may use at most 64 MiB of HBM per device.

v0:
```python
import jax
import jax.numpy as jnp
from jax import lax
from jax.sharding import Mesh
from jax.sharding import PartitionSpec as P

ITERS = 3
DOM = ("dom_0", "dom_1", "dom_2", "dom_3")


def passed_along(block, axis, distance):
    devices = range(lax.axis_size(axis))
    route = [(i - distance, i) for i in devices if i - distance in devices]
    return lax.ppermute(block, axis, route)


def one_axis_at_a_time(x, axes):
    for axis in axes:
        x = lax.psum(x, axis)
    return x


def inner_sum(first, second):
    return jnp.sum(first * second, axis=1)


def on_device(currents, conductance, ground, ell_cols, send_rows):
    link_count, bound_width = send_rows.shape
    reach_span = link_count // 2
    offsets = list(range(-reach_span, 0)) + list(range(1, reach_span + 1))

    def place_of(offset):
        return offset + reach_span if offset < 0 else offset + reach_span - 1

    live_send = send_rows >= 0
    send_index = jnp.where(live_send, send_rows, 0)
    outgoing_cond = jnp.where(live_send, conductance[send_index], 0.0)
    cond_regions = []
    for position, offset in enumerate(offsets):
        cond_regions.append(passed_along(outgoing_cond[link_count - 1 - position], DOM, -offset))
    extended_cond = jnp.concatenate([conductance] + cond_regions)
    present = ell_cols >= 0
    columns = jnp.where(present, ell_cols, 0)
    weight = jnp.where(present, 0.5 * (conductance[None, :] + extended_cond[columns]), 0.0)
    degree = ground + jnp.sum(weight, axis=0)
    slot_count = ell_cols.shape[0]

    def boundary(field):
        outgoing = jnp.where(live_send[None], field[:, send_index], 0.0)
        regions = [None] * link_count
        for heading in (1, -1):
            carried = jnp.stack(
                [outgoing[:, place_of(heading * distance)] for distance in range(1, reach_span + 1)]
            )
            for distance in range(1, reach_span + 1):
                arrived = passed_along(carried, DOM, heading)
                regions[place_of(-heading * distance)] = arrived[0]
                carried = arrived[1:]
        return jnp.concatenate([field] + regions, axis=1)

    def operate(field):
        extended = boundary(field)
        beside = jnp.zeros_like(field)
        for slot_index in range(slot_count):
            beside = beside + weight[slot_index][None, :] * extended[:, columns[slot_index]]
        return degree[None, :] * field - beside

    voltages = jnp.zeros_like(currents)
    residual = currents
    applied = operate(residual)
    direction = residual
    image_direction = applied
    curve_direction = applied
    norm_old = None
    step_old = None
    for iteration in range(ITERS):
        norm_now, cross_term = (
            one_axis_at_a_time(inner_sum(residual, residual), DOM),
            one_axis_at_a_time(inner_sum(applied, residual), DOM),
        )
        more_steps = iteration + 1 < ITERS
        if more_steps:
            product = operate(applied)
        if iteration == 0:
            step_size = norm_now / cross_term
            direction = residual
            image_direction = applied
            curve_direction = product
        else:
            beta_ratio = norm_now / norm_old
            step_size = norm_now / (cross_term - beta_ratio * norm_now / step_old)
            direction = residual + beta_ratio[:, None] * direction
            image_direction = applied + beta_ratio[:, None] * image_direction
            if more_steps:
                curve_direction = product + beta_ratio[:, None] * curve_direction
        voltages = voltages + step_size[:, None] * direction
        residual = residual - step_size[:, None] * image_direction
        if more_steps:
            applied = applied - step_size[:, None] * curve_direction
        norm_old = norm_now
        step_old = step_size
    return (voltages, residual)


def solution(mesh):
    finer = Mesh(mesh.devices.reshape(4, 4, 8, 2), ("dom_0", "dom_1", "dom_2", "dom_3"))
    placed = (P(None, DOM), P(DOM), P(DOM), P(None, DOM), P(DOM, None))
    return jax.shard_map(
        on_device,
        mesh=finer,
        in_specs=placed,
        out_specs=(P(None, DOM), P(None, DOM)),
        check_vma=False,
    )
```

profile of v0, /device:TPU:1, one launch (start us, length us, event | category | flops | bytes accessed | tf_op | source)
XLA Modules:
  0.0 544.6 jit_solution(3076656520024255696)
XLA Ops:
  40.3 101.8 %gather_fusion.1 = f32[18432]{0:T(1024)S(1)} fusion(f32[2816]{0:T(1024)S(1)} %constant_dynamic-update-slice_fusion.22, s32[18432]{0:T(1024)S(1)} %broadcast_clamp_fusion), kind=kCustom, calls=%fused_computation.1 | custom fusion | bytes 221184 | tf_op jit(solution)/shard_map/gather | solution.py:44
  162.6 5.5 %gather_fusion.5 = f32[2048,16]{1,0:T(8,128)S(1)} fusion(f32[16,2816]{0,1:T(8,128)S(1)} %copy.103, s32[2048]{0:T(1024)S(1)} %get-tuple-element.109), kind=kCustom, calls=%fused_computation.5 | custom fusion | bytes 270336 | tf_op jit(solution)/shard_map/gather | solution.py:65
  168.3 5.5 %gather_fusion.6 = f32[2048,16]{1,0:T(8,128)S(1)} fusion(f32[16,2816]{0,1:T(8,128)S(1)} %copy.103, s32[2048]{0:T(1024)S(1)} %get-tuple-element.108), kind=kCustom, calls=%fused_computation.6 | custom fusion | bytes 270336 | tf_op jit(solution)/shard_map/gather | solution.py:65
  174.1 5.5 %gather_fusion.7 = f32[2048,16]{1,0:T(8,128)S(1)} fusion(f32[16,2816]{0,1:T(8,128)S(1)} %copy.103, s32[2048]{0:T(1024)S(1)} %get-tuple-element.107), kind=kCustom, calls=%fused_computation.7 | custom fusion | bytes 270336 | tf_op jit(solution)/shard_map/gather | solution.py:65
  179.9 5.5 %gather_fusion.8 = f32[2048,16]{1,0:T(8,128)S(1)} fusion(f32[16,2816]{0,1:T(8,128)S(1)} %copy.103, s32[2048]{0:T(1024)S(1)} %get-tuple-element.106), kind=kCustom, calls=%fused_computation.8 | custom fusion | bytes 270336 | tf_op jit(solution)/shard_map/gather | solution.py:65
  185.7 5.5 %gather_fusion.9 = f32[2048,16]{1,0:T(8,128)S(1)} fusion(f32[16,2816]{0,1:T(8,128)S(1)} %copy.103, s32[2048]{0:T(1024)S(1)} %get-tuple-element.105), kind=kCustom, calls=%fused_computation.9 | custom fusion | bytes 270336 | tf_op jit(solution)/shard_map/gather | solution.py:65
  191.5 5.5 %gather_fusion.10 = f32[2048,16]{1,0:T(8,128)S(1)} fusion(f32[16,2816]{0,1:T(8,128)S(1)} %copy.103, s32[2048]{0:T(1024)S(1)} %copy-done.38), kind=kCustom, calls=%fused_computation.10 | custom fusion | bytes 270336 | tf_op jit(solution)/shard_map/gather | solution.py:65
  227.6 23.6 %all-reduce.8 = (f32[16]{0:T(128)S(1)}, f32[16]{0:T(128)S(1)}) all-reduce(f32[16]{0:T(128)S(1)} %get-tuple-element.15, f32[16]{0:T(128)S(1)} %get-tuple-element.14), channel_id=1, replica_groups=mesh['dom_0'=4,'dom_1'=4,'dom_2'=8,'dom_3'=2] {'dom_0'}, use_global_device_ids=true, to_apply=%region_1.2 | all-reduce | flops 32 | bytes 256 | tf_op jit(solution)/shard_map/psum | solution.py:19
  251.2 6.0 %all-reduce.5 = (f32[16]{0:T(128)S(1)}, f32[16]{0:T(128)S(1)}) all-reduce(f32[16]{0:T(128)S(1)} %get-tuple-element.32, f32[16]{0:T(128)S(1)} %get-tuple-element.33), channel_id=1, replica_groups=mesh['dom_0'=4,'dom_1'=4,'dom_2'=8,'dom_3'=2] {'dom_1'}, use_global_device_ids=true, to_apply=%region_2.3 | all-reduce | flops 32 | bytes 256 | tf_op jit(solution)/shard_map/psum | solution.py:19
  257.2 21.0 %all-reduce.2 = (f32[16]{0:T(128)S(1)}, f32[16]{0:T(128)S(1)}) all-reduce(f32[16]{0:T(128)S(1)} %get-tuple-element.26, f32[16]{0:T(128)S(1)} %get-tuple-element.27), channel_id=1, replica_groups=mesh['dom_0'=4,'dom_1'=4,'dom_2'=8,'dom_3'=2] {'dom_2'}, use_global_device_ids=true, to_apply=%region_3.4 | all-reduce | flops 32 | bytes 256 | tf_op jit(solution)/shard_map/psum | solution.py:19
  289.4 7.6 %gather_fusion.14 = f32[2048,16]{1,0:T(8,128)} fusion(f32[16,2816]{0,1:T(8,128)S(1)} %copy.123, s32[2048]{0:T(1024)S(1)} %copy-done.27), kind=kCustom, calls=%fused_computation.14 | custom fusion | bytes 270336 | tf_op jit(solution)/shard_map/gather | solution.py:65
  297.0 7.6 %gather_fusion.15 = f32[2048,16]{1,0:T(8,128)} fusion(f32[16,2816]{0,1:T(8,128)S(1)} %copy.123, s32[2048]{0:T(1024)S(1)} %copy-done.25), kind=kCustom, calls=%fused_computation.15 | custom fusion | bytes 270336 | tf_op jit(solution)/shard_map/gather | solution.py:65
  304.6 7.6 %gather_fusion.16 = f32[2048,16]{1,0:T(8,128)} fusion(f32[16,2816]{0,1:T(8,128)S(1)} %copy.123, s32[2048]{0:T(1024)S(1)} %copy-done.31), kind=kCustom, calls=%fused_computation.16 | custom fusion | bytes 270336 | tf_op jit(solution)/shard_map/gather | solution.py:65
  312.2 7.6 %gather_fusion.17 = f32[2048,16]{1,0:T(8,128)} fusion(f32[16,2816]{0,1:T(8,128)S(1)} %copy.123, s32[2048]{0:T(1024)S(1)} %copy-done.29), kind=kCustom, calls=%fused_computation.17 | custom fusion | bytes 270336 | tf_op jit(solution)/shard_map/gather | solution.py:65
  319.7 7.6 %gather_fusion.18 = f32[2048,16]{1,0:T(8,128)} fusion(f32[16,2816]{0,1:T(8,128)S(1)} %copy.123, s32[2048]{0:T(1024)S(1)} %copy-done.37), kind=kCustom, calls=%fused_computation.18 | custom fusion | bytes 270336 | tf_op jit(solution)/shard_map/gather | solution.py:65
  327.3 7.6 %gather_fusion.19 = f32[2048,16]{1,0:T(8,128)} fusion(f32[16,2816]{0,1:T(8,128)S(1)} %copy.123, s32[2048]{0:T(1024)S(1)} %copy-done.33), kind=kCustom, calls=%fused_computation.19 | custom fusion | bytes 270336 | tf_op jit(solution)/shard_map/gather | solution.py:65
  334.9 7.6 %gather_fusion.20 = f32[2048,16]{1,0:T(8,128)} fusion(f32[16,2816]{0,1:T(8,128)S(1)} %copy.123, s32[2048]{0:T(1024)S(1)} %copy-done.39), kind=kCustom, calls=%fused_computation.20 | custom fusion | bytes 270336 | tf_op jit(solution)/shard_map/gather | solution.py:65
  342.4 7.6 %gather_fusion.13 = f32[2048,16]{1,0:T(8,128)} fusion(f32[16,2816]{0,1:T(8,128)S(1)} %copy.123, s32[2048]{0:T(1024)S(1)} %copy-done.23), kind=kCustom, calls=%fused_computation.13 | custom fusion | bytes 270336 | tf_op jit(solution)/shard_map/gather | solution.py:65
  376.3 6.9 %all-reduce.7 = (f32[16]{0:T(128)S(1)}, f32[16]{0:T(128)S(1)}) all-reduce(f32[16]{0:T(128)S(1)} %get-tuple-element.13, f32[16]{0:T(128)S(1)} %get-tuple-element.12), channel_id=1, replica_groups=mesh['dom_0'=4,'dom_1'=4,'dom_2'=8,'dom_3'=2] {'dom_0'}, use_global_device_ids=true, to_apply=%region_12.13 | all-reduce | flops 32 | bytes 256 | tf_op jit(solution)/shard_map/psum | solution.py:19
  383.3 7.1 %all-reduce.4 = (f32[16]{0:T(128)S(1)}, f32[16]{0:T(128)S(1)}) all-reduce(f32[16]{0:T(128)S(1)} %get-tuple-element.30, f32[16]{0:T(128)S(1)} %get-tuple-element.31), channel_id=1, replica_groups=mesh['dom_0'=4,'dom_1'=4,'dom_2'=8,'dom_3'=2] {'dom_1'}, use_global_device_ids=true, to_apply=%region_13.14 | all-reduce | flops 32 | bytes 256 | tf_op jit(solution)/shard_map/psum | solution.py:19
  390.3 20.2 %all-reduce.1 = (f32[16]{0:T(128)S(1)}, f32[16]{0:T(128)S(1)}) all-reduce(f32[16]{0:T(128)S(1)} %get-tuple-element.24, f32[16]{0:T(128)S(1)} %get-tuple-element.25), channel_id=1, replica_groups=mesh['dom_0'=4,'dom_1'=4,'dom_2'=8,'dom_3'=2] {'dom_2'}, use_global_device_ids=true, to_apply=%region_14.15 | all-reduce | flops 32 | bytes 256 | tf_op jit(solution)/shard_map/psum | solution.py:19
  432.7 7.6 %gather_fusion.25 = f32[2048,16]{1,0:T(8,128)} fusion(f32[16,2816]{0,1:T(8,128)S(1)} %copy.143, s32[2048]{0:T(1024)S(1)} %copy-done.25), kind=kCustom, calls=%fused_computation.25 | custom fusion | bytes 270336 | tf_op jit(solution)/shard_map/gather | solution.py:65
  440.3 7.6 %gather_fusion.26 = f32[2048,16]{1,0:T(8,128)} fusion(f32[16,2816]{0,1:T(8,128)S(1)} %copy.143, s32[2048]{0:T(1024)S(1)} %copy-done.31), kind=kCustom, calls=%fused_computation.26 | custom fusion | bytes 270336 | tf_op jit(solution)/shard_map/gather | solution.py:65
  447.9 7.6 %gather_fusion.27 = f32[2048,16]{1,0:T(8,128)} fusion(f32[16,2816]{0,1:T(8,128)S(1)} %copy.143, s32[2048]{0:T(1024)S(1)} %copy-done.29), kind=kCustom, calls=%fused_computation.27 | custom fusion | bytes 270336 | tf_op jit(solution)/shard_map/gather | solution.py:65
  455.4 7.6 %gather_fusion.28 = f32[2048,16]{1,0:T(8,128)} fusion(f32[16,2816]{0,1:T(8,128)S(1)} %copy.143, s32[2048]{0:T(1024)S(1)} %copy-done.37), kind=kCustom, calls=%fused_computation.28 | custom fusion | bytes 270336 | tf_op jit(solution)/shard_map/gather | solution.py:65
  463.0 7.6 %gather_fusion.29 = f32[2048,16]{1,0:T(8,128)} fusion(f32[16,2816]{0,1:T(8,128)S(1)} %copy.143, s32[2048]{0:T(1024)S(1)} %copy-done.33), kind=kCustom, calls=%fused_computation.29 | custom fusion | bytes 270336 | tf_op jit(solution)/shard_map/gather | solution.py:65
  470.6 7.6 %gather_fusion.30 = f32[2048,16]{1,0:T(8,128)} fusion(f32[16,2816]{0,1:T(8,128)S(1)} %copy.143, s32[2048]{0:T(1024)S(1)} %copy-done.40), kind=kCustom, calls=%fused_computation.30 | custom fusion | bytes 270336 | tf_op jit(solution)/shard_map/gather | solution.py:65
  478.1 7.6 %gather_fusion.23 = f32[2048,16]{1,0:T(8,128)} fusion(f32[16,2816]{0,1:T(8,128)S(1)} %copy.143, s32[2048]{0:T(1024)S(1)} %copy-done.23), kind=kCustom, calls=%fused_computation.23 | custom fusion | bytes 270336 | tf_op jit(solution)/shard_map/gather | solution.py:65
  485.7 7.6 %gather_fusion.31 = f32[2048,16]{1,0:T(8,128)} fusion(f32[16,2816]{0,1:T(8,128)S(1)} %copy.143, s32[2048]{0:T(1024)S(1)} %copy-done.35), kind=kCustom, calls=%fused_computation.31 | custom fusion | bytes 270336 | tf_op jit(solution)/shard_map/gather | solution.py:65
  504.7 7.7 %all-reduce.6 = (f32[16]{0:T(128)S(1)}, f32[16]{0:T(128)S(1)}) all-reduce(f32[16]{0:T(128)S(1)} %get-tuple-element.11, f32[16]{0:T(128)S(1)} %get-tuple-element.10), channel_id=1, replica_groups=mesh['dom_0'=4,'dom_1'=4,'dom_2'=8,'dom_3'=2] {'dom_0'}, use_global_device_ids=true, to_apply=%region_22.23 | all-reduce | flops 32 | bytes 256 | tf_op jit(solution)/shard_map/psum | solution.py:19
  512.4 6.0 %all-reduce.3 = (f32[16]{0:T(128)S(1)}, f32[16]{0:T(128)S(1)}) all-reduce(f32[16]{0:T(128)S(1)} %get-tuple-element.28, f32[16]{0:T(128)S(1)} %get-tuple-element.29), channel_id=1, replica_groups=mesh['dom_0'=4,'dom_1'=4,'dom_2'=8,'dom_3'=2] {'dom_1'}, use_global_device_ids=true, to_apply=%region_23.24 | all-reduce | flops 32 | bytes 256 | tf_op jit(solution)/shard_map/psum | solution.py:19
  518.4 20.6 %all-reduce = (f32[16]{0:T(128)S(1)}, f32[16]{0:T(128)S(1)}) all-reduce(f32[16]{0:T(128)S(1)} %get-tuple-element.22, f32[16]{0:T(128)S(1)} %get-tuple-element.23), channel_id=1, replica_groups=mesh['dom_0'=4,'dom_1'=4,'dom_2'=8,'dom_3'=2] {'dom_2'}, use_global_device_ids=true, to_apply=%region_24.25 | all-reduce | flops 32 | bytes 256 | tf_op jit(solution)/shard_map/psum | solution.py:19
  (290 shorter events, 168.0 us)
Async XLA Ops:
  4.4 137.8 %collective-permute-start.6 = (f32[3,16,128]{2,1,0:T(8,128)S(1)}, f32[3,16,128]{2,1,0:T(8,128)S(1)}, u32[]{:S(2)}, u32[]{:S(2)}) collective-permute-start(f32[3,16,128]{2,1,0:T(8,128)S(1)} %pad_maximum_fusion), channel_id=1, source_target_pairs={{0,1},{1,2},{2,3},{3,4},{4,5},{5,6},{6,7},{7,8},{8,9},{9,10},{10,1... | collective-permute-start | bytes 73736 | tf_op jit(solution)/shard_map/ppermute | solution.py:14
  9.3 135.2 %collective-permute-start.9 = (f32[3,16,128]{2,1,0:T(8,128)S(1)}, f32[3,16,128]{2,1,0:T(8,128)S(1)}, u32[]{:S(2)}, u32[]{:S(2)}) collective-permute-start(f32[3,16,128]{2,1,0:T(8,128)S(1)} %pad_maximum_fusion.1), channel_id=1, source_target_pairs={{1,0},{2,1},{3,2},{4,3},{5,4},{6,5},{7,6},{8,7},{9,8},{10,9},{11,1... | collective-permute-start | bytes 73736 | tf_op jit(solution)/shard_map/ppermute | solution.py:14
  15.9 13.4 %collective-permute-start = (f32[128]{0:T(128)S(1)}, f32[128]{0:T(128)S(1)}, u32[]{:S(2)}, u32[]{:S(2)}) collective-permute-start(f32[128]{0:T(128)S(1)} %get-tuple-element.102), channel_id=1, source_target_pairs={{0,3},{1,4},{2,5},{3,6},{4,7},{5,8},{6,9},{7,10},{8,11},{9,12},{10... | collective-permute-start | bytes 1544 | tf_op jit(solution)/shard_map/ppermute | solution.py:14
  20.9 10.3 %collective-permute-start.1 = (f32[128]{0:T(128)S(1)}, f32[128]{0:T(128)S(1)}, u32[]{:S(2)}, u32[]{:S(2)}) collective-permute-start(f32[128]{0:T(128)S(1)} %get-tuple-element.101), channel_id=1, source_target_pairs={{0,2},{1,3},{2,4},{3,5},{4,6},{5,7},{6,8},{7,9},{8,10},{9,11},{10,... | collective-permute-start | bytes 1544 | tf_op jit(solution)/shard_map/ppermute | solution.py:14
  24.5 8.1 %collective-permute-start.2 = (f32[128]{0:T(128)S(1)}, f32[128]{0:T(128)S(1)}, u32[]{:S(2)}, u32[]{:S(2)}) collective-permute-start(f32[128]{0:T(128)S(1)} %get-tuple-element.100), channel_id=1, source_target_pairs={{0,1},{1,2},{2,3},{3,4},{4,5},{5,6},{6,7},{7,8},{8,9},{9,10},{10,1... | collective-permute-start | bytes 1544 | tf_op jit(solution)/shard_map/ppermute | solution.py:14
  28.5 175.8 %copy-start.22 = (s32[2048]{0:T(1024)}, s32[2048]{0:T(1024)S(1)}, u32[]{:S(2)}) copy-start(s32[2048]{0:T(1024)S(1)} %broadcast_clamp_fusion.9) | copy-start | bytes 24580
  28.6 128.2 %copy-start.26 = (s32[2048]{0:T(1024)}, s32[2048]{0:T(1024)S(1)}, u32[]{:S(2)}) copy-start(s32[2048]{0:T(1024)S(1)} %get-tuple-element.110) | copy-start | bytes 24580
  28.6 133.9 %copy-start.24 = (s32[2048]{0:T(1024)}, s32[2048]{0:T(1024)S(1)}, u32[]{:S(2)}) copy-start(s32[2048]{0:T(1024)S(1)} %get-tuple-element.109) | copy-start | bytes 24580
  28.6 139.7 %copy-start.30 = (s32[2048]{0:T(1024)}, s32[2048]{0:T(1024)S(1)}, u32[]{:S(2)}) copy-start(s32[2048]{0:T(1024)S(1)} %get-tuple-element.108) | copy-start | bytes 24580
  28.6 145.5 %copy-start.28 = (s32[2048]{0:T(1024)}, s32[2048]{0:T(1024)S(1)}, u32[]{:S(2)}) copy-start(s32[2048]{0:T(1024)S(1)} %get-tuple-element.107) | copy-start | bytes 24580
  28.7 151.2 %copy-start.36 = (s32[2048]{0:T(1024)}, s32[2048]{0:T(1024)S(1)}, u32[]{:S(2)}) copy-start(s32[2048]{0:T(1024)S(1)} %get-tuple-element.106) | copy-start | bytes 24580
  28.7 157.0 %copy-start.32 = (s32[2048]{0:T(1024)}, s32[2048]{0:T(1024)S(1)}, u32[]{:S(2)}) copy-start(s32[2048]{0:T(1024)S(1)} %get-tuple-element.105) | copy-start | bytes 24580
  29.3 5.6 %collective-permute-start.3 = (f32[128]{0:T(128)S(1)}, f32[128]{0:T(128)S(1)}, u32[]{:S(2)}, u32[]{:S(2)}) collective-permute-start(f32[128]{0:T(128)S(1)} %get-tuple-element.99), channel_id=1, source_target_pairs={{1,0},{2,1},{3,2},{4,3},{5,4},{6,5},{7,6},{8,7},{9,8},{10,9},{11,1... | collective-permute-start | bytes 1544 | tf_op jit(solution)/shard_map/ppermute | solution.py:14
  31.2 5.5 %collective-permute-start.4 = (f32[128]{0:T(128)S(1)}, f32[128]{0:T(128)S(1)}, u32[]{:S(2)}, u32[]{:S(2)}) collective-permute-start(f32[128]{0:T(128)S(1)} %get-tuple-element.98), channel_id=1, source_target_pairs={{2,0},{3,1},{4,2},{5,3},{6,4},{7,5},{8,6},{9,7},{10,8},{11,9},{12,... | collective-permute-start | bytes 1544 | tf_op jit(solution)/shard_map/ppermute | solution.py:14
  32.6 7.7 %collective-permute-start.5 = (f32[128]{0:T(128)S(1)}, f32[128]{0:T(128)S(1)}, u32[]{:S(2)}, u32[]{:S(2)}) collective-permute-start(f32[128]{0:T(128)S(1)} %get-tuple-element.97), channel_id=1, source_target_pairs={{3,0},{4,1},{5,2},{6,3},{7,4},{8,5},{9,6},{10,7},{11,8},{12,9},{13... | collective-permute-start | bytes 1544 | tf_op jit(solution)/shard_map/ppermute | solution.py:14
  40.3 110.5 %copy-start.47 = (f32[2048]{0:T(1024)S(1)}, f32[2048]{0:T(1024)}, u32[]{:S(2)}) copy-start(f32[2048]{0:T(1024)} %param.7) | copy-start | bytes 24580
  142.1 4.4 collective-permute-start.7
  144.5 6.9 %collective-permute-start.10 = (f32[2,16,128]{2,1,0:T(8,128)S(1)}, f32[2,16,128]{2,1,0:T(8,128)S(1)}, u32[]{:S(2)}, u32[]{:S(2)}) collective-permute-start(f32[2,16,128]{2,1,0:T(8,128)S(1)} %slice.376), channel_id=1, source_target_pairs={{1,0},{2,1},{3,2},{4,3},{5,4},{6,5},{7,6},{8,7},{9,8},{10,9},{11,1... | collective-permute-start | bytes 49160 | tf_op jit(solution)/shard_map/ppermute | solution.py:14
  146.6 6.7 %collective-permute-start.8 = (f32[1,16,128]{2,1,0:T(8,128)S(1)}, f32[1,16,128]{2,1,0:T(8,128)S(1)}, u32[]{:S(2)}, u32[]{:S(2)}) collective-permute-start(f32[1,16,128]{2,1,0:T(8,128)S(1)} %slice.369), channel_id=1, source_target_pairs={{0,1},{1,2},{2,3},{3,4},{4,5},{5,6},{6,7},{7,8},{8,9},{9,10},{10,1... | collective-permute-start | bytes 24584 | tf_op jit(solution)/shard_map/ppermute | solution.py:14
  151.4 5.0 collective-permute-start.11
  213.4 4.4 collective-permute-start.12
  215.5 6.3 %collective-permute-start.15 = (f32[3,16,128]{2,1,0:T(8,128)S(1)}, f32[3,16,128]{2,1,0:T(8,128)S(1)}, u32[]{:S(2)}, u32[]{:S(2)}) collective-permute-start(f32[3,16,128]{2,1,0:T(8,128)S(1)} %pad_maximum_fusion.3), channel_id=1, source_target_pairs={{1,0},{2,1},{3,2},{4,3},{5,4},{6,5},{7,6},{8,7},{9,8},{10,9},{11,1... | collective-permute-start | bytes 73736 | tf_op jit(solution)/shard_map/ppermute | solution.py:14
  217.8 6.0 %collective-permute-start.13 = (f32[2,16,128]{2,1,0:T(8,128)S(1)}, f32[2,16,128]{2,1,0:T(8,128)S(1)}, u32[]{:S(2)}, u32[]{:S(2)}) collective-permute-start(f32[2,16,128]{2,1,0:T(8,128)S(1)} %slice.399), channel_id=1, source_target_pairs={{0,1},{1,2},{2,3},{3,4},{4,5},{5,6},{6,7},{7,8},{8,9},{9,10},{10,1... | collective-permute-start | bytes 49160 | tf_op jit(solution)/shard_map/ppermute | solution.py:14
  221.9 61.9 %collective-permute-start.16 = (f32[2,16,128]{2,1,0:T(8,128)S(1)}, f32[2,16,128]{2,1,0:T(8,128)S(1)}, u32[]{:S(2)}, u32[]{:S(2)}) collective-permute-start(f32[2,16,128]{2,1,0:T(8,128)S(1)} %slice.407), channel_id=1, source_target_pairs={{1,0},{2,1},{3,2},{4,3},{5,4},{6,5},{7,6},{8,7},{9,8},{10,9},{11,1... | collective-permute-start | bytes 49160 | tf_op jit(solution)/shard_map/ppermute | solution.py:14
  223.8 62.2 %collective-permute-start.14 = (f32[1,16,128]{2,1,0:T(8,128)S(1)}, f32[1,16,128]{2,1,0:T(8,128)S(1)}, u32[]{:S(2)}, u32[]{:S(2)}) collective-permute-start(f32[1,16,128]{2,1,0:T(8,128)S(1)} %slice.400), channel_id=1, source_target_pairs={{0,1},{1,2},{2,3},{3,4},{4,5},{5,6},{6,7},{7,8},{8,9},{9,10},{10,1... | collective-permute-start | bytes 24584 | tf_op jit(solution)/shard_map/ppermute | solution.py:14
  283.8 5.2 collective-permute-start.17
  368.4 4.4 collective-permute-start.18
  370.4 44.8 %collective-permute-start.21 = (f32[3,16,128]{2,1,0:T(8,128)S(1)}, f32[3,16,128]{2,1,0:T(8,128)S(1)}, u32[]{:S(2)}, u32[]{:S(2)}) collective-permute-start(f32[3,16,128]{2,1,0:T(8,128)S(1)} %pad_maximum_fusion.5), channel_id=1, source_target_pairs={{1,0},{2,1},{3,2},{4,3},{5,4},{6,5},{7,6},{8,7},{9,8},{10,9},{11,1... | collective-permute-start | bytes 73736 | tf_op jit(solution)/shard_map/ppermute | solution.py:14
  372.8 44.9 %collective-permute-start.19 = (f32[2,16,128]{2,1,0:T(8,128)S(1)}, f32[2,16,128]{2,1,0:T(8,128)S(1)}, u32[]{:S(2)}, u32[]{:S(2)}) collective-permute-start(f32[2,16,128]{2,1,0:T(8,128)S(1)} %slice.413), channel_id=1, source_target_pairs={{0,1},{1,2},{2,3},{3,4},{4,5},{5,6},{6,7},{7,8},{8,9},{9,10},{10,1... | collective-permute-start | bytes 49160 | tf_op jit(solution)/shard_map/ppermute | solution.py:14
  415.2 6.6 %collective-permute-start.22 = (f32[2,16,128]{2,1,0:T(8,128)S(1)}, f32[2,16,128]{2,1,0:T(8,128)S(1)}, u32[]{:S(2)}, u32[]{:S(2)}) collective-permute-start(f32[2,16,128]{2,1,0:T(8,128)S(1)} %slice.421), channel_id=1, source_target_pairs={{1,0},{2,1},{3,2},{4,3},{5,4},{6,5},{7,6},{8,7},{9,8},{10,9},{11,1... | collective-permute-start | bytes 49160 | tf_op jit(solution)/shard_map/ppermute | solution.py:14
  417.7 6.1 %collective-permute-start.20 = (f32[1,16,128]{2,1,0:T(8,128)S(1)}, f32[1,16,128]{2,1,0:T(8,128)S(1)}, u32[]{:S(2)}, u32[]{:S(2)}) collective-permute-start(f32[1,16,128]{2,1,0:T(8,128)S(1)} %slice.414), channel_id=1, source_target_pairs={{0,1},{1,2},{2,3},{3,4},{4,5},{5,6},{6,7},{7,8},{8,9},{9,10},{10,1... | collective-permute-start | bytes 24584 | tf_op jit(solution)/shard_map/ppermute | solution.py:14
  421.9 5.0 collective-permute-start.23
  (51 other events, 681.7 us)
where the time goes:
time: 546 us; the launch traced here: 545 us
  local copies, waits for them, and re-layouts  320 us (59%)
  blocking collectives  133 us (24%)
  starting transfers between devices  65.3 us (12%)
  waiting for transfers between devices  15.3 us (3%)
  other arithmetic  8.55 us (2%)
    gather x54, local copies, waits for them, and re-layouts, operate(): extended[:, columns[slot_index]]  198 us
    psum x12, blocking collectives, one_axis_at_a_time(): x = lax.psum(x, axis)  133 us
    gather x2, local copies, waits for them, and re-layouts, on_device(): extended_cond[columns]  102 us
    ppermute x24, starting transfers between devices, passed_along(): return lax.ppermute(block, axis, route)  65.3 us
    ppermute x24, waiting for transfers between devices, passed_along(): return lax.ppermute(block, axis, route)  15.3 us
  transfers between devices with their start and end apart: 24, of which 6 were waited for; matrix products, arithmetic and copies ran while one was open for 20% of the time, Pallas kernels for 0%

commit v1 on v0

v1 whole, which is shorter than its diff:
```python
import functools

import jax
import jax.numpy as jnp
from jax import lax
from jax.experimental import pallas as pl
from jax.experimental.pallas import tpu as pltpu
from jax.sharding import PartitionSpec as P

MESH = pl.DeviceIdType.MESH
F32, BF16, I16, I32 = jnp.float32, jnp.bfloat16, jnp.int16, jnp.int32
LANES = 128
WIDE = 256


def pieces(x):
    high = x.astype(BF16)
    rest = x - high.astype(F32)
    mid = rest.astype(BF16)
    low = (rest - mid.astype(F32)).astype(BF16)
    return [high, mid, low]


def joined(y, first, rows):
    return (y[first + 2 * rows : first + 3 * rows] + y[first + rows : first + 2 * rows]) + y[first : first + rows]


def tiles(width):
    return [slice(i, i + LANES) for i in range(0, width, LANES)]


def kernel(
    parts, group, cur, cond, gnd, ell, send, volt, resid,
    adj, sel, v1, v2, v3, y0, y1, y2, diag, lhs, blhs, slhs, wsend, u0, u1, u2, t0, t1, t2,
    out0, out1, out2, in0, in1, in2, red, ex_send, ex_recv, red_send, red_recv,
):
    pairs, nodes = cur.shape
    slots = ell.shape[0]
    links = send.shape[0]
    bound = links * LANES
    reach = links // 2
    offsets = list(range(-reach, 0)) + list(range(1, reach + 1))
    me = lax.axis_index("dom")
    others = parts // group
    mine, place = me // group, me % group

    neighbours = [lax.rem(me + e + parts, parts) for e in offsets]
    near = [mine * group + lax.rem(place + d, group) for d in range(1, group)]
    far = [lax.rem(mine + d, others) * group + place for d in range(1, others)]

    barrier = pltpu.get_barrier_semaphore()
    for peer in neighbours + near + far:
        pl.semaphore_signal(barrier, inc=1, device_id={"dom": peer}, device_id_type=MESH)

    ones = jnp.ones((16, LANES), BF16)
    none = jnp.zeros((16, LANES), BF16)
    row_ids = lax.broadcasted_iota(I32, (16, LANES), 0).astype(I16)

    def spread(row):
        return jnp.broadcast_to(row, (16, LANES)).astype(I16)

    for o in range(links):
        listed = spread(send[o : o + 1, :])

        def fill_sel(i, _, listed=listed, o=o):
            for q in range(16):
                at = pl.multiple_of(i * 256 + q * 16, 16)
                ids = row_ids + at.astype(I16)
                sel[pl.ds(at, 16), o * LANES : (o + 1) * LANES] = jnp.where(listed == ids, ones, none)
            return 0

        lax.fori_loop(0, nodes // 256, fill_sel, 0)

    def picked(y_parts, rows):
        for i, piece in enumerate(y_parts):
            slhs[i * rows : (i + 1) * rows, :] = piece

    slhs[...] = jnp.zeros_like(slhs)
    picked(pieces(cur[...]), pairs)
    for i, piece in enumerate(pieces(cond[...])):
        slhs[3 * pairs + i : 3 * pairs + i + 1, :] = piece
    for b in range(0, bound, WIDE):
        y = jnp.dot(slhs[...], sel[:, b : b + WIDE], preferred_element_type=F32)
        u0[:, b : b + WIDE] = joined(y, 0, pairs)
        c_part = joined(y, 3 * pairs, 1)
        wsend[:, b : b + WIDE] = jnp.broadcast_to(c_part, (8, WIDE))
    for o in range(links):
        s = slice(o * LANES, (o + 1) * LANES)
        out0[o, 0:pairs, :] = u0[:, s]
        out0[o, pairs : pairs + 8, :] = wsend[:, s]

    def exchange(step, out, into):
        copies = []
        for o in range(links):
            copies.append(
                pltpu.make_async_remote_copy(
                    src_ref=out.at[o],
                    dst_ref=into.at[links - 1 - o],
                    send_sem=ex_send.at[step, o],
                    recv_sem=ex_recv.at[step, links - 1 - o],
                    device_id={"dom": neighbours[o]},
                    device_id_type=MESH,
                )
            )
        return copies

    def start(copies):
        for copy in copies:
            copy.start()

    def arrive(copies):
        for copy in copies:
            copy.wait_recv()

    pl.semaphore_wait(barrier, len(neighbours) + len(near) + len(far))
    ex0 = exchange(0, out0, in0)
    start(ex0)

    def build(t, _):
        off = pl.multiple_of(t * LANES, LANES)
        block = ell[:, pl.ds(off, LANES)]
        cols = [spread(block[s : s + 1, :]) for s in range(slots)]
        counts = []
        for s in range(slots):
            total = none
            for other in range(slots):
                total = total + jnp.where(cols[s] == cols[other], ones, none)
            counts.append(total)

        def fill(i, _):
            for q in range(16):
                at = pl.multiple_of(i * 256 + q * 16, 16)
                ids = row_ids + at.astype(I16)
                acc = none
                for s in range(slots):
                    acc = jnp.where(cols[s] == ids, counts[s], acc)
                adj[pl.ds(at, 16), pl.ds(off, LANES)] = acc
            return 0

        lax.fori_loop(0, nodes // 256, fill, 0)

        remote = spread(jnp.max(block, axis=0, keepdims=True))

        def fill_remote(i, _):
            for q in range(16):
                at = pl.multiple_of(nodes + i * 256 + q * 16, 16)
                ids = row_ids + at.astype(I16)
                adj[pl.ds(at, 16), pl.ds(off, LANES)] = jnp.where(remote == ids, ones, none)
            return 0

        lax.fori_loop(0, bound // 256, fill_remote, 0)
        return 0

    lax.fori_loop(0, nodes // LANES, build, 0)

    def split_field(v):
        for i, piece in enumerate(pieces(v)):
            lhs[i * pairs : (i + 1) * pairs, :] = piece
        for i, piece in enumerate(pieces(v * cond[...])):
            lhs[(3 + i) * pairs : (4 + i) * pairs, :] = piece

    half = 0.5

    def local_operator(v, y, first):
        rows = 7 * pairs if first else 6 * pairs
        for b in range(0, nodes, WIDE):
            s = slice(b, b + WIDE)
            prod = jnp.dot(lhs[0:rows, :], adj[0:nodes, s], preferred_element_type=F32)
            c = cond[:, s]
            if first:
                extra = prod[6 * pairs :]
                around = joined(extra, 0, 1)
                diag[:, s] = gnd[:, s] + half * (c * extra[3:4] + around)
            y[:, s] = diag[:, s] * v[:, s] - half * (c * joined(prod, 0, pairs) + joined(prod, 3 * pairs, pairs))

    def pick_listed(y, start_with):
        picked(pieces(y[...]), pairs)
        got = []
        for b in range(0, bound, WIDE):
            prod = jnp.dot(slhs[0 : 3 * pairs, :], sel[:, b : b + WIDE], preferred_element_type=F32)
            got.append(joined(prod, 0, pairs))
        return got

    def add_received(t, y, v):
        for i, piece in enumerate(pieces(t[...])):
            blhs[i * pairs : (i + 1) * pairs, :] = piece
        for b in range(0, nodes, WIDE):
            s = slice(b, b + WIDE)
            prod = jnp.dot(blhs[...], adj[nodes:, s], preferred_element_type=F32)
            v[:, s] = y[:, s] + joined(prod, 0, pairs)

    def lane_sums(first, second):
        total = None
        for s in tiles(first.shape[1]):
            term = first[:, s] * second[:, s]
            total = term if total is None else total + term
        return total

    def row_of(sums):
        blocks = jnp.concatenate(sums + [jnp.zeros((LANES - pairs * len(sums), LANES), F32)], axis=0)
        return jnp.sum(jnp.transpose(blocks), axis=0, keepdims=True)

    def reduction(stage, peers):
        copies = []
        for d, peer in enumerate(peers, start=1):
            copies.append(
                pltpu.make_async_remote_copy(
                    src_ref=red.at[stage, 0],
                    dst_ref=red.at[stage, d],
                    send_sem=red_send.at[stage, d],
                    recv_sem=red_recv.at[stage, d],
                    device_id={"dom": peer},
                    device_id_type=MESH,
                )
            )
        return copies

    def summed(stage, count):
        terms = [red[stage, d] for d in range(count)]
        while len(terms) > 1:
            terms = [a + b for a, b in zip(terms[0::2], terms[1::2], strict=True)]
        return terms[0]

    def spread_row(row):
        return jnp.transpose(jnp.broadcast_to(row, (LANES, LANES)))

    lhs[6 * pairs :, :] = jnp.zeros((pairs, nodes), BF16)
    for i, piece in enumerate(pieces(cond[...])):
        lhs[6 * pairs + i : 6 * pairs + i + 1, :] = piece
    lhs[6 * pairs + 3 : 6 * pairs + 4, :] = jnp.ones((1, nodes), BF16)
    split_field(cur[...])
    local_operator(cur, y0, True)
    m0 = lane_sums(cur, cur)
    m1 = lane_sums(cur, y0)
    ys = pick_listed(y0, None)

    def pass_on(u, into, t, ys, u_next, out):
        for o in range(links):
            s = slice(o * LANES, (o + 1) * LANES)
            term = wsend[:, s]
            term = jnp.concatenate([term] * (pairs // 8), axis=0) * (u[:, s] - into[o, 0:pairs, :])
            t[:, s] = term
            if u_next is not None:
                inner = s.start % WIDE
                nxt = ys[s.start // WIDE][:, inner : inner + LANES] + term
                u_next[:, s] = nxt
                out[o, :, :] = nxt

    arrive(ex0)
    for o in range(links):
        s = slice(o * LANES, (o + 1) * LANES)
        live = jnp.broadcast_to(send[o : o + 1, :], (8, LANES)) >= 0
        wsend[:, s] = jnp.where(live, half * (wsend[:, s] + in0[o, pairs : pairs + 8, :]), 0.0)
    pass_on(u0, in0, t0, ys, u1, out1)
    ex1 = exchange(1, out1, in1)
    start(ex1)
    m1 = m1 + lane_sums(u0, t0)
    red[0, 0] = row_of([m0, m1])
    near0 = reduction(0, near)
    start(near0)

    add_received(t0, y0, v1)
    split_field(v1[...])
    local_operator(v1, y1, False)
    ys = pick_listed(y1, None)

    arrive(ex1)
    pass_on(u1, in1, t1, ys, u2, out2)
    ex2 = exchange(2, out2, in2)
    start(ex2)
    arrive(near0)
    red[1, 0] = summed(0, group)
    far0 = reduction(1, far)
    start(far0)

    add_received(t1, y1, v2)
    split_field(v2[...])
    local_operator(v2, y2, False)

    arrive(ex2)
    pass_on(u2, in2, t2, None, None, None)
    arrive(far0)
    first_sums = spread_row(summed(1, others))
    m0, m1 = first_sums[0:pairs], first_sums[pairs : 2 * pairs]
    a0 = m0 / m1

    zero = jnp.zeros((pairs, LANES), F32)
    k0, k1, k2, k3 = zero, zero, zero, zero
    for s in tiles(nodes):
        r1 = cur[:, s] - a0 * v1[:, s]
        q1 = v1[:, s] - a0 * v2[:, s]
        k0 = k0 + r1 * r1
        k1 = k1 + r1 * q1
        k2 = k2 + q1 * q1
        k3 = k3 + q1 * (y1[:, s] - a0 * y2[:, s])
    for s in tiles(bound):
        k3 = k3 + (u1[:, s] - a0 * u2[:, s]) * (t1[:, s] - a0 * t2[:, s])
    red[2, 0] = row_of([k0, k1, k2, k3])
    near1 = reduction(2, near)
    start(near1)

    add_received(t2, y2, v3)

    arrive(near1)
    red[3, 0] = summed(2, group)
    far1 = reduction(3, far)
    start(far1)
    arrive(far1)
    sums = spread_row(summed(3, others))
    k0, k1, k2, k3 = (sums[i * pairs : (i + 1) * pairs] for i in range(4))

    b1 = k0 / m0
    a1 = k0 / (k1 - b1 * k0 / a0)
    v1q1 = -(k0 / a0 + k1) / a0
    r2q1 = k1 - a1 * (k2 + b1 * v1q1)
    rr2 = -a1 * r2q1
    b2 = rr2 / k0
    v1q2 = (v1q1 - k2) / a0
    r2q2 = k2 - a1 * (k3 + b1 * v1q2)
    r2ar2 = r2q1 - a1 * (r2q2 - b1 * r2q1 / a0)
    a2 = rr2 / (r2ar2 - b2 * rr2 / a1)

    for s in tiles(nodes):
        w0, w1, w2, w3 = cur[:, s], v1[:, s], v2[:, s], v3[:, s]
        r1 = w0 - a0 * w1
        q1 = w1 - a0 * w2
        q2 = w2 - a0 * w3
        p1 = r1 + b1 * w0
        ap1 = q1 + b1 * w1
        r2 = r1 - a1 * ap1
        ar2 = q1 - a1 * (q2 + b1 * w2)
        p2 = r2 + b2 * p1
        ap2 = ar2 + b2 * ap1
        volt[:, s] = a0 * w0 + a1 * p1 + a2 * p2
        resid[:, s] = r2 - a2 * ap2

    for copies in (ex0, ex1, ex2, near0, far0, near1, far1):
        for copy in copies:
            copy.wait_send()


def solve(parts, group, currents, conductance, ground, ell_cols, send_rows):
    pairs, nodes = currents.shape
    links = send_rows.shape[0]
    bound = links * LANES
    others = parts // group
    most = max(group, others)
    field = pltpu.VMEM((pairs, nodes), F32)
    edge = pltpu.VMEM((pairs, bound), F32)
    vmem = pl.BlockSpec(memory_space=pltpu.VMEM)
    return pl.pallas_call(
        functools.partial(kernel, parts, group),
        out_shape=(jax.ShapeDtypeStruct((pairs, nodes), F32),) * 2,
        in_specs=[vmem] * 5,
        out_specs=(vmem, vmem),
        scratch_shapes=[
            pltpu.VMEM((nodes + bound, nodes), BF16),
            pltpu.VMEM((nodes, bound), BF16),
            field, field, field, field, field, field,
            pltpu.VMEM((1, nodes), F32),
            pltpu.VMEM((7 * pairs, nodes), BF16),
            pltpu.VMEM((3 * pairs, bound), BF16),
            pltpu.VMEM((4 * pairs, nodes), BF16),
            pltpu.VMEM((8, bound), F32),
            edge, edge, edge, edge, edge, edge,
            pltpu.VMEM((links, pairs + 8, LANES), F32),
            pltpu.VMEM((links, pairs, LANES), F32),
            pltpu.VMEM((links, pairs, LANES), F32),
            pltpu.VMEM((links, pairs + 8, LANES), F32),
            pltpu.VMEM((links, pairs, LANES), F32),
            pltpu.VMEM((links, pairs, LANES), F32),
            pltpu.VMEM((4, most, 1, LANES), F32),
            pltpu.SemaphoreType.DMA((3, links)),
            pltpu.SemaphoreType.DMA((3, links)),
            pltpu.SemaphoreType.DMA((4, most)),
            pltpu.SemaphoreType.DMA((4, most)),
        ],
        compiler_params=pltpu.CompilerParams(
            collective_id=0, has_side_effects=True, vmem_limit_bytes=48 * 1024 * 1024
        ),
    )(currents, conductance.reshape(1, nodes), ground.reshape(1, nodes), ell_cols, send_rows)


def solution(mesh):
    parts = mesh.shape["dom"]
    group = 16 if parts >= 256 else 4
    placed = (P(None, "dom"), P("dom"), P("dom"), P(None, "dom"), P("dom", None))
    return jax.shard_map(
        functools.partial(solve, parts, group),
        mesh=mesh,
        in_specs=placed,
        out_specs=(P(None, "dom"), P(None, "dom")),
        check_vma=False,
    )
```

time: 546 us -> 48.7 us (0.09)
  local copies, waits for them, and re-layouts: 320 us -> 5.19 us
  blocking collectives: 133 us -> 0 us
  starting transfers between devices: 65.3 us -> 0 us
  Pallas kernels: 0 us -> 42.6 us
  waiting for transfers between devices: 15.3 us -> 0 us
  other arithmetic: 8.55 us -> 0 us
    gather x63 -> x0, local copies, waits for them, and re-layouts: 309 us -> none  [the longest x54 198 us: operate(): extended[:, columns[slot_index]]]
    psum x12 -> x0, blocking collectives: 133 us -> none  [one_axis_at_a_time(): x = lax.psum(x, axis)]
    ppermute x24 -> x0, starting transfers between devices: 65.3 us -> none  [passed_along(): return lax.ppermute(block, axis, route)]
    pallas_call x0 -> x1, Pallas kernels: none -> 42.6 us  [solve(): pl.pallas_call(functools.partial(kernel, parts, group), out_shape=(jax.Sh...]
    ppermute x24 -> x0, waiting for transfers between devices: 15.3 us -> none  [passed_along(): return lax.ppermute(block, axis, route)]
  transfers between devices with their start and end apart: 24 -> 0, of which waited for: 6 -> 0; matrix products, arithmetic and copies ran while one was open for 20% -> 0% of each run, Pallas kernels for 0% -> 0%
where the time goes in v1:
time: 48.7 us; the launch traced here: 48.5 us
  Pallas kernels  42.6 us (87%)
  local copies, waits for them, and re-layouts  5.19 us (11%)
  between operations  0.65 us (1%)
    pallas_call x1, Pallas kernels, solve(): pl.pallas_call(functools.partial(kernel, parts, group), out_shape=(jax.Sh...  42.6 us
    unnamed x12, local copies, waits for them, and re-layouts  5.19 us

profile of v1, /device:TPU:1, one launch (start us, length us, event | category | flops | bytes accessed | tf_op | source)
XLA Modules:
  0.0 48.5 jit_solution(17361489082810031127)
XLA Ops:
  0.6 0.0 copy-start
  0.6 0.9 %copy-done = f32[16,2048]{1,0:T(8,128)S(1)} copy-done((f32[16,2048]{1,0:T(8,128)S(1)}, f32[16,2048]{1,0:T(8,128)}, u32[]{:S(2)}) %copy-start) | copy-done | bytes 131096
  1.5 0.0 copy-start.1
  1.5 0.9 %copy-done.1 = s32[9,2048]{1,0:T(8,128)S(1)} copy-done((s32[9,2048]{1,0:T(8,128)S(1)}, s32[9,2048]{1,0:T(8,128)}, u32[]{:S(2)}) %copy-start.1) | copy-done | bytes 73752
  2.4 0.0 copy-start.2
  2.4 0.7 %copy-done.2 = f32[2048]{0:T(1024)S(1)} copy-done((f32[2048]{0:T(1024)S(1)}, f32[2048]{0:T(1024)}, u32[]{:S(2)}) %copy-start.2) | copy-done | bytes 8216
  3.1 0.0 copy-start.3
  3.1 0.7 %copy-done.3 = f32[2048]{0:T(1024)S(1)} copy-done((f32[2048]{0:T(1024)S(1)}, f32[2048]{0:T(1024)}, u32[]{:S(2)}) %copy-start.3) | copy-done | bytes 8216
  3.8 0.0 copy-start.4
  3.8 0.7 %copy-done.4 = s32[6,128]{1,0:T(8,128)S(1)} copy-done((s32[6,128]{1,0:T(8,128)S(1)}, s32[6,128]{1,0:T(8,128)}, u32[]{:S(2)}) %copy-start.4) | copy-done | bytes 3096
  4.5 42.6 %shard_map.68 = (f32[16,2048]{1,0:T(8,128)S(1)}, f32[16,2048]{1,0:T(8,128)S(1)}) custom-call(f32[16,2048]{1,0:T(8,128)S(1)} %copy-done, f32[1,2048]{1,0:T(1,128)S(1)} %bitcast.2, f32[1,2048]{1,0:T(1,128)S(1)} %bitcast.3, s32[9,2048]{1,0:T(8,128)S(1)} %copy-done.1, s32[6,128]{1,0:T(8,128)S(1)} %copy-done.4), custom_call_target="tpu_custom_call" | custom-call | tf_op jit(solution)/shard_map/pallas_call | solution.py:351
  47.2 0.7 %copy.9 = f32[16,2048]{1,0:T(8,128)} copy(f32[16,2048]{1,0:T(8,128)S(1)} %get-tuple-element.4) | data formatting | bytes 262144
  47.8 0.7 %copy.10 = f32[16,2048]{1,0:T(8,128)} copy(f32[16,2048]{1,0:T(8,128)S(1)} %get-tuple-element.5) | data formatting | bytes 262144
Async XLA Ops:
  0.6 0.9 %copy-start = (f32[16,2048]{1,0:T(8,128)S(1)}, f32[16,2048]{1,0:T(8,128)}, u32[]{:S(2)}) copy-start(f32[16,2048]{1,0:T(8,128)} %cur.1) | copy-start | bytes 393220
  1.5 0.9 %copy-start.1 = (s32[9,2048]{1,0:T(8,128)S(1)}, s32[9,2048]{1,0:T(8,128)}, u32[]{:S(2)}) copy-start(s32[9,2048]{1,0:T(8,128)} %ell.1) | copy-start | bytes 221188
  2.4 0.7 %copy-start.2 = (f32[2048]{0:T(1024)S(1)}, f32[2048]{0:T(1024)}, u32[]{:S(2)}) copy-start(f32[2048]{0:T(1024)} %param.6) | copy-start | bytes 24580
  3.1 0.7 %copy-start.3 = (f32[2048]{0:T(1024)S(1)}, f32[2048]{0:T(1024)}, u32[]{:S(2)}) copy-start(f32[2048]{0:T(1024)} %param.7) | copy-start | bytes 24580
  3.8 0.7 %copy-start.4 = (s32[6,128]{1,0:T(8,128)S(1)}, s32[6,128]{1,0:T(8,128)}, u32[]{:S(2)}) copy-start(s32[6,128]{1,0:T(8,128)} %send.1) | copy-start | bytes 9220

commit v2 on v1

--- a/solution.py
+++ b/solution.py
@@ -11,6 +11,7 @@
 F32, BF16, I16, I32 = jnp.float32, jnp.bfloat16, jnp.int16, jnp.int32
 LANES = 128
 WIDE = 256
+DIGITS = 8
 
 
 def pieces(x):
@@ -30,8 +31,8 @@
 
 
 def kernel(
-    parts, group, cur, cond, gnd, ell, send, volt, resid,
-    adj, sel, v1, v2, v3, y0, y1, y2, diag, lhs, blhs, slhs, wsend, u0, u1, u2, t0, t1, t2,
+    parts, group, cur_in, cond_in, gnd_in, ell_in, send_in, volt, resid,
+    cur, cond, gnd, ell, send, in_sem, adj, sel, v1, v2, v3, y0, y1, y2, diag, lhs, blhs, slhs, wsend, u0, u1, u2, t0, t1, t2,
     out0, out1, out2, in0, in1, in2, red, ex_send, ex_recv, red_send, red_recv,
 ):
     pairs, nodes = cur.shape
@@ -48,6 +49,16 @@
     near = [mine * group + lax.rem(place + d, group) for d in range(1, group)]
     far = [lax.rem(mine + d, others) * group + place for d in range(1, others)]
 
+    loads = [
+        pltpu.make_async_copy(source, target, in_sem.at[i])
+        for i, (source, target) in enumerate(
+            ((cur_in, cur), (cond_in, cond), (gnd_in, gnd), (ell_in, ell), (send_in, send))
+        )
+    ]
+    loads[4].start()
+    loads[0].start()
+    for i in range(1, 4):
+        loads[i].start()
     barrier = pltpu.get_barrier_semaphore()
     for peer in neighbours + near + far:
         pl.semaphore_signal(barrier, inc=1, device_id={"dom": peer}, device_id_type=MESH)
@@ -55,32 +66,36 @@
     ones = jnp.ones((16, LANES), BF16)
     none = jnp.zeros((16, LANES), BF16)
     row_ids = lax.broadcasted_iota(I32, (16, LANES), 0).astype(I16)
+    word_ids = lax.broadcasted_iota(I32, (8, LANES), 0)
+    no_word = jnp.zeros((8, LANES), I32)
+    words = nodes // DIGITS
 
     def spread(row):
         return jnp.broadcast_to(row, (16, LANES)).astype(I16)
 
-    for o in range(links):
-        listed = spread(send[o : o + 1, :])
-
-        def fill_sel(i, _, listed=listed, o=o):
-            for q in range(16):
-                at = pl.multiple_of(i * 256 + q * 16, 16)
-                ids = row_ids + at.astype(I16)
-                sel[pl.ds(at, 16), o * LANES : (o + 1) * LANES] = jnp.where(listed == ids, ones, none)
-            return 0
-
-        lax.fori_loop(0, nodes // 256, fill_sel, 0)
+    with jax.named_scope("selbuild"):
+        loads[4].wait()
+        listed = [spread(send[o : o + 1, :]) for o in range(links)]
+        for at in range(0, nodes, 16):
+            ids = row_ids + jnp.int16(at)
+            for o in range(links):
+                sel[o, at : at + 16, :] = jnp.where(listed[o] == ids, ones, none)
+
+    def sel_block(b):
+        return jnp.concatenate([sel[b // LANES], sel[b // LANES + 1]], axis=1)
 
     def picked(y_parts, rows):
         for i, piece in enumerate(y_parts):
             slhs[i * rows : (i + 1) * rows, :] = piece
 
+    loads[0].wait()
+    loads[1].wait()
     slhs[...] = jnp.zeros_like(slhs)
     picked(pieces(cur[...]), pairs)
     for i, piece in enumerate(pieces(cond[...])):
         slhs[3 * pairs + i : 3 * pairs + i + 1, :] = piece
     for b in range(0, bound, WIDE):
-        y = jnp.dot(slhs[...], sel[:, b : b + WIDE], preferred_element_type=F32)
+        y = jnp.dot(slhs[...], sel_block(b), preferred_element_type=F32)
         u0[:, b : b + WIDE] = joined(y, 0, pairs)
         c_part = joined(y, 3 * pairs, 1)
         wsend[:, b : b + WIDE] = jnp.broadcast_to(c_part, (8, WIDE))
@@ -112,60 +127,69 @@
         for copy in copies:
             copy.wait_recv()
 
-    pl.semaphore_wait(barrier, len(neighbours) + len(near) + len(far))
-    ex0 = exchange(0, out0, in0)
-    start(ex0)
-
     def build(t, _):
         off = pl.multiple_of(t * LANES, LANES)
         block = ell[:, pl.ds(off, LANES)]
-        cols = [spread(block[s : s + 1, :]) for s in range(slots)]
-        counts = []
-        for s in range(slots):
-            total = none
-            for other in range(slots):
-                total = total + jnp.where(cols[s] == cols[other], ones, none)
-            counts.append(total)
-
-        def fill(i, _):
-            for q in range(16):
-                at = pl.multiple_of(i * 256 + q * 16, 16)
-                ids = row_ids + at.astype(I16)
-                acc = none
+        local = (block >= 0) & (block < nodes)
+        wide_g = jnp.where(local, block & (words - 1), -1)
+        wide_p = jnp.left_shift(jnp.ones_like(block), jnp.where(local, (block // words) * 4, 0))
+        g = [jnp.broadcast_to(wide_g[s : s + 1, :], (8, LANES)) for s in range(slots)]
+        p = [jnp.broadcast_to(wide_p[s : s + 1, :], (8, LANES)) for s in range(slots)]
+        word = list(p)
+        for i in range(slots):
+            for j in range(i):
+                same = g[i] == g[j]
+                word[i] = word[i] + jnp.where(same, p[j], no_word)
+                word[j] = word[j] + jnp.where(same, p[i], no_word)
+        for h in range(0, words, 64):
+            chunk = []
+            for q in range(h, h + 64, 8):
+                ids = word_ids + q
+                acc = no_word
                 for s in range(slots):
-                    acc = jnp.where(cols[s] == ids, counts[s], acc)
-                adj[pl.ds(at, 16), pl.ds(off, LANES)] = acc
-            return 0
-
-        lax.fori_loop(0, nodes // 256, fill, 0)
-
+                    acc = jnp.where(g[s] == ids, word[s], acc)
+                chunk.append(acc)
+            chunk = jnp.concatenate(chunk, axis=0)
+            for r in range(DIGITS):
+                last = r == DIGITS - 1
+                digit = lax.shift_right_logical(chunk, 4 * r) if last else chunk & (15 << (4 * r))
+                adj[t, r * words + h : r * words + h + 64, :] = digit.astype(F32).astype(BF16)
         remote = spread(jnp.max(block, axis=0, keepdims=True))
-
-        def fill_remote(i, _):
-            for q in range(16):
-                at = pl.multiple_of(nodes + i * 256 + q * 16, 16)
-                ids = row_ids + at.astype(I16)
-                adj[pl.ds(at, 16), pl.ds(off, LANES)] = jnp.where(remote == ids, ones, none)
-            return 0
-
-        lax.fori_loop(0, bound // 256, fill_remote, 0)
+        for at in range(nodes, nodes + bound, 16):
+            adj[t, at : at + 16, :] = jnp.where(remote == row_ids + jnp.int16(at), ones, none)
         return 0
 
-    lax.fori_loop(0, nodes // LANES, build, 0)
+    def adj_block(b, first, last):
+        return jnp.concatenate([adj[b // LANES, first:last, :], adj[b // LANES + 1, first:last, :]], axis=1)
+
+    def scale_of(r):
+        return 1.0 if r == DIGITS - 1 else 16.0**-r
 
     def split_field(v):
-        for i, piece in enumerate(pieces(v)):
-            lhs[i * pairs : (i + 1) * pairs, :] = piece
-        for i, piece in enumerate(pieces(v * cond[...])):
-            lhs[(3 + i) * pairs : (4 + i) * pairs, :] = piece
+        for r in range(DIGITS):
+            s = slice(r * words, (r + 1) * words)
+            part = v[:, s] * scale_of(r)
+            for i, piece in enumerate(pieces(part)):
+                lhs[i * pairs : (i + 1) * pairs, s] = piece
+            for i, piece in enumerate(pieces(part * cond[:, s])):
+                lhs[(3 + i) * pairs : (4 + i) * pairs, s] = piece
 
     half = 0.5
+    with jax.named_scope("adj_a"):
+        loads[3].wait()
+        lax.fori_loop(0, nodes // LANES // 2, build, 0)
+    with jax.named_scope("barwait"):
+        pl.semaphore_wait(barrier, len(neighbours) + len(near) + len(far))
+    ex0 = exchange(0, out0, in0)
+    start(ex0)
+    with jax.named_scope("adj_b"):
+        lax.fori_loop(nodes // LANES // 2, nodes // LANES, build, 0)
 
     def local_operator(v, y, first):
         rows = 7 * pairs if first else 6 * pairs
         for b in range(0, nodes, WIDE):
             s = slice(b, b + WIDE)
-            prod = jnp.dot(lhs[0:rows, :], adj[0:nodes, s], preferred_element_type=F32)
+            prod = jnp.dot(lhs[0:rows, :], adj_block(b, 0, nodes), preferred_element_type=F32)
             c = cond[:, s]
             if first:
                 extra = prod[6 * pairs :]
@@ -177,7 +201,7 @@
         picked(pieces(y[...]), pairs)
         got = []
         for b in range(0, bound, WIDE):
-            prod = jnp.dot(slhs[0 : 3 * pairs, :], sel[:, b : b + WIDE], preferred_element_type=F32)
+            prod = jnp.dot(slhs[0 : 3 * pairs, :], sel_block(b), preferred_element_type=F32)
             got.append(joined(prod, 0, pairs))
         return got
 
@@ -186,7 +210,7 @@
             blhs[i * pairs : (i + 1) * pairs, :] = piece
         for b in range(0, nodes, WIDE):
             s = slice(b, b + WIDE)
-            prod = jnp.dot(blhs[...], adj[nodes:, s], preferred_element_type=F32)
+            prod = jnp.dot(blhs[...], adj_block(b, nodes, nodes + bound), preferred_element_type=F32)
             v[:, s] = y[:, s] + joined(prod, 0, pairs)
 
     def lane_sums(first, second):
@@ -225,10 +249,13 @@
         return jnp.transpose(jnp.broadcast_to(row, (LANES, LANES)))
 
     lhs[6 * pairs :, :] = jnp.zeros((pairs, nodes), BF16)
-    for i, piece in enumerate(pieces(cond[...])):
-        lhs[6 * pairs + i : 6 * pairs + i + 1, :] = piece
-    lhs[6 * pairs + 3 : 6 * pairs + 4, :] = jnp.ones((1, nodes), BF16)
-    split_field(cur[...])
+    loads[2].wait()
+    for r in range(DIGITS):
+        s = slice(r * words, (r + 1) * words)
+        for i, piece in enumerate(pieces(cond[:, s] * scale_of(r))):
+            lhs[6 * pairs + i : 6 * pairs + i + 1, s] = piece
+        lhs[6 * pairs + 3 : 6 * pairs + 4, s] = jnp.full((1, words), scale_of(r), BF16)
+    split_field(cur)
     local_operator(cur, y0, True)
     m0 = lane_sums(cur, cur)
     m1 = lane_sums(cur, y0)
@@ -260,7 +287,7 @@
     start(near0)
 
     add_received(t0, y0, v1)
-    split_field(v1[...])
+    split_field(v1)
     local_operator(v1, y1, False)
     ys = pick_listed(y1, None)
 
@@ -274,7 +301,7 @@
     start(far0)
 
     add_received(t1, y1, v2)
-    split_field(v2[...])
+    split_field(v2)
     local_operator(v2, y2, False)
 
     arrive(ex2)
@@ -339,6 +366,14 @@
             copy.wait_send()
 
 
+def write_out(volt, resid, volt_out, resid_out, sems):
+    copies = [pltpu.make_async_copy(volt, volt_out, sems.at[0]), pltpu.make_async_copy(resid, resid_out, sems.at[1])]
+    for copy in copies:
+        copy.start()
+    for copy in copies:
+        copy.wait()
+
+
 def solve(parts, group, currents, conductance, ground, ell_cols, send_rows):
     pairs, nodes = currents.shape
     links = send_rows.shape[0]
@@ -348,14 +383,20 @@
     field = pltpu.VMEM((pairs, nodes), F32)
     edge = pltpu.VMEM((pairs, bound), F32)
     vmem = pl.BlockSpec(memory_space=pltpu.VMEM)
-    return pl.pallas_call(
+    volt, resid = pl.pallas_call(
         functools.partial(kernel, parts, group),
         out_shape=(jax.ShapeDtypeStruct((pairs, nodes), F32),) * 2,
-        in_specs=[vmem] * 5,
+        in_specs=[pl.BlockSpec(memory_space=pltpu.HBM)] * 5,
         out_specs=(vmem, vmem),
         scratch_shapes=[
-            pltpu.VMEM((nodes + bound, nodes), BF16),
-            pltpu.VMEM((nodes, bound), BF16),
+            field,
+            pltpu.VMEM((1, nodes), F32),
+            pltpu.VMEM((1, nodes), F32),
+            pltpu.VMEM(ell_cols.shape, I32),
+            pltpu.VMEM(send_rows.shape, I32),
+            pltpu.SemaphoreType.DMA((5,)),
+            pltpu.VMEM((nodes // LANES, nodes + bound, LANES), BF16),
+            pltpu.VMEM((links, nodes, LANES), BF16),
             field, field, field, field, field, field,
             pltpu.VMEM((1, nodes), F32),
             pltpu.VMEM((7 * pairs, nodes), BF16),
@@ -378,7 +419,15 @@
         compiler_params=pltpu.CompilerParams(
             collective_id=0, has_side_effects=True, vmem_limit_bytes=48 * 1024 * 1024
         ),
-    )(currents, conductance.reshape(1, nodes), ground.reshape(1, nodes), ell_cols, send_rows)
+    )(*(pltpu.with_memory_space_constraint(x, pltpu.HBM) for x in (currents, conductance.reshape(1, nodes), ground.reshape(1, nodes), ell_cols, send_rows)))
+    return pl.pallas_call(
+        write_out,
+        out_shape=(jax.ShapeDtypeStruct((pairs, nodes), F32),) * 2,
+        in_specs=[vmem] * 2,
+        out_specs=(pl.BlockSpec(memory_space=pltpu.HBM),) * 2,
+        scratch_shapes=[pltpu.SemaphoreType.DMA((2,))],
+        compiler_params=pltpu.CompilerParams(vmem_limit_bytes=1 << 20),
+    )(volt, resid)
 
 
 def solution(mesh):

time: 48.7 us -> 38.2 us (0.78)
  local copies, waits for them, and re-layouts: 5.19 us -> 0 us
  Pallas kernels: 42.6 us -> 37.5 us
    pallas_call x1, Pallas kernels: 42.6 us -> 36.7 us  [solve(): pl.pallas_call(functools.partial(kernel, parts, group), out_shape=(jax.Sh...]
    unnamed x12 -> x0, local copies, waits for them, and re-layouts: 5.19 us -> none
    pallas_call x0 -> x1, Pallas kernels: none -> 0.72 us  [solve(): pl.pallas_call(write_out, out_shape=(jax.ShapeDtypeStruct((pairs, nodes),...]
where the time goes in v2:
time: 38.2 us; the launch traced here: 38.1 us
  Pallas kernels  37.5 us (98%)
  between operations  0.64 us (2%)
    pallas_call x1, Pallas kernels, solve(): pl.pallas_call(functools.partial(kernel, parts, group), out_shape=(jax.Sh...  36.7 us

profile of v2, /device:TPU:1, one launch (start us, length us, event | category | flops | bytes accessed | tf_op | source)
XLA Modules:
  0.0 38.1 jit_solution(3094147283500822986)
XLA Ops:
  0.6 36.7 %shard_map.68 = (f32[16,2048]{1,0:T(8,128)S(1)}, f32[16,2048]{1,0:T(8,128)S(1)}) custom-call(f32[16,2048]{1,0:T(8,128)} %cur_in.1, f32[1,2048]{1,0:T(1,128)} %bitcast.2, f32[1,2048]{1,0:T(1,128)} %bitcast.3, s32[9,2048]{1,0:T(8,128)} %ell_in.1, s32[6,128]{1,0:T(8,128)} %send_in.1), custom_call_target="tpu_custom_call" | custom-call | tf_op jit(solution)/shard_map/pallas_call | solution.py:386
  37.4 0.7 %shard_map.69 = (f32[16,2048]{1,0:T(8,128)}, f32[16,2048]{1,0:T(8,128)}) custom-call(f32[16,2048]{1,0:T(8,128)S(1)} %get-tuple-element.4.volt, f32[16,2048]{1,0:T(8,128)S(1)} %get-tuple-element.5.resid), custom_call_target="tpu_custom_call" | custom-call | tf_op jit(solution)/shard_map/pallas_call | solution.py:423

commit v3 on v2

--- a/solution.py
+++ b/solution.py
@@ -45,10 +45,24 @@
     others = parts // group
     mine, place = me // group, me % group
 
-    neighbours = [lax.rem(me + e + parts, parts) for e in offsets]
+    assert reach == 3
+    neighbours, landing = [], []
+    for o, e in enumerate(offsets):
+        d = abs(e)
+        edge = me if e < 0 else parts - 1 - me
+        spare = jnp.where(edge == 0, 1 if d < 3 else 2, 0)
+        spare_d = jnp.where(edge == 0, min(d + 1, 3), jnp.where(edge == 1, d - 1, 3))
+        inside = edge >= d
+        spare_peer = spare if e < 0 else parts - 1 - spare
+        spare_slot = reach - spare_d if e < 0 else reach - 1 + spare_d
+        neighbours.append(jnp.where(inside, me + e, spare_peer))
+        landing.append(jnp.where(inside, links - 1 - o, spare_slot))
     near = [mine * group + lax.rem(place + d, group) for d in range(1, group)]
     far = [lax.rem(mine + d, others) * group + place for d in range(1, others)]
 
+    barrier = pltpu.get_barrier_semaphore()
+    for peer in neighbours + near + far:
+        pl.semaphore_signal(barrier, inc=1, device_id={"dom": peer}, device_id_type=MESH)
     loads = [
         pltpu.make_async_copy(source, target, in_sem.at[i])
         for i, (source, target) in enumerate(
@@ -59,9 +73,6 @@
     loads[0].start()
     for i in range(1, 4):
         loads[i].start()
-    barrier = pltpu.get_barrier_semaphore()
-    for peer in neighbours + near + far:
-        pl.semaphore_signal(barrier, inc=1, device_id={"dom": peer}, device_id_type=MESH)
 
     ones = jnp.ones((16, LANES), BF16)
     none = jnp.zeros((16, LANES), BF16)
@@ -105,27 +116,19 @@
         out0[o, pairs : pairs + 8, :] = wsend[:, s]
 
     def exchange(step, out, into):
-        copies = []
         for o in range(links):
-            copies.append(
-                pltpu.make_async_remote_copy(
-                    src_ref=out.at[o],
-                    dst_ref=into.at[links - 1 - o],
-                    send_sem=ex_send.at[step, o],
-                    recv_sem=ex_recv.at[step, links - 1 - o],
-                    device_id={"dom": neighbours[o]},
-                    device_id_type=MESH,
-                )
-            )
-        return copies
-
-    def start(copies):
-        for copy in copies:
-            copy.start()
-
-    def arrive(copies):
-        for copy in copies:
-            copy.wait_recv()
+            pltpu.make_async_remote_copy(
+                src_ref=out.at[o],
+                dst_ref=into.at[landing[o]],
+                send_sem=ex_send.at[step],
+                recv_sem=ex_recv.at[step],
+                device_id={"dom": neighbours[o]},
+                device_id_type=MESH,
+            ).start()
+        return pltpu.make_async_remote_copy(
+            src_ref=out, dst_ref=into, send_sem=ex_send.at[step], recv_sem=ex_recv.at[step],
+            device_id={"dom": neighbours[0]}, device_id_type=MESH,
+        )
 
     def build(t, _):
         off = pl.multiple_of(t * LANES, LANES)
@@ -177,13 +180,13 @@
     half = 0.5
     with jax.named_scope("adj_a"):
         loads[3].wait()
-        lax.fori_loop(0, nodes // LANES // 2, build, 0)
+        ahead = jnp.where(place < group // 2, nodes // LANES, nodes // LANES // 4)
+        lax.fori_loop(0, ahead, build, 0)
     with jax.named_scope("barwait"):
         pl.semaphore_wait(barrier, len(neighbours) + len(near) + len(far))
     ex0 = exchange(0, out0, in0)
-    start(ex0)
     with jax.named_scope("adj_b"):
-        lax.fori_loop(nodes // LANES // 2, nodes // LANES, build, 0)
+        lax.fori_loop(ahead, nodes // LANES, build, 0)
 
     def local_operator(v, y, first):
         rows = 7 * pairs if first else 6 * pairs
@@ -225,19 +228,20 @@
         return jnp.sum(jnp.transpose(blocks), axis=0, keepdims=True)
 
     def reduction(stage, peers):
-        copies = []
         for d, peer in enumerate(peers, start=1):
-            copies.append(
-                pltpu.make_async_remote_copy(
-                    src_ref=red.at[stage, 0],
-                    dst_ref=red.at[stage, d],
-                    send_sem=red_send.at[stage, d],
-                    recv_sem=red_recv.at[stage, d],
-                    device_id={"dom": peer},
-                    device_id_type=MESH,
-                )
-            )
-        return copies
+            pltpu.make_async_remote_copy(
+                src_ref=red.at[stage, 0],
+                dst_ref=red.at[stage, d],
+                send_sem=red_send.at[stage],
+                recv_sem=red_recv.at[stage],
+                device_id={"dom": peer},
+                device_id_type=MESH,
+            ).start()
+        slots_used = red.at[stage, 1 : len(peers) + 1]
+        return pltpu.make_async_remote_copy(
+            src_ref=slots_used, dst_ref=slots_used, send_sem=red_send.at[stage], recv_sem=red_recv.at[stage],
+            device_id={"dom": peers[0]}, device_id_type=MESH,
+        )
 
     def summed(stage, count):
         terms = [red[stage, d] for d in range(count)]
@@ -273,40 +277,36 @@
                 u_next[:, s] = nxt
                 out[o, :, :] = nxt
 
-    arrive(ex0)
+    ex0.wait_recv()
     for o in range(links):
         s = slice(o * LANES, (o + 1) * LANES)
         live = jnp.broadcast_to(send[o : o + 1, :], (8, LANES)) >= 0
         wsend[:, s] = jnp.where(live, half * (wsend[:, s] + in0[o, pairs : pairs + 8, :]), 0.0)
     pass_on(u0, in0, t0, ys, u1, out1)
     ex1 = exchange(1, out1, in1)
-    start(ex1)
     m1 = m1 + lane_sums(u0, t0)
     red[0, 0] = row_of([m0, m1])
     near0 = reduction(0, near)
-    start(near0)
 
     add_received(t0, y0, v1)
     split_field(v1)
     local_operator(v1, y1, False)
     ys = pick_listed(y1, None)
 
-    arrive(ex1)
+    ex1.wait_recv()
     pass_on(u1, in1, t1, ys, u2, out2)
     ex2 = exchange(2, out2, in2)
-    start(ex2)
-    arrive(near0)
+    near0.wait_recv()
     red[1, 0] = summed(0, group)
     far0 = reduction(1, far)
-    start(far0)
 
     add_received(t1, y1, v2)
     split_field(v2)
     local_operator(v2, y2, False)
 
-    arrive(ex2)
+    ex2.wait_recv()
     pass_on(u2, in2, t2, None, None, None)
-    arrive(far0)
+    far0.wait_recv()
     first_sums = spread_row(summed(1, others))
     m0, m1 = first_sums[0:pairs], first_sums[pairs : 2 * pairs]
     a0 = m0 / m1
@@ -324,15 +324,13 @@
         k3 = k3 + (u1[:, s] - a0 * u2[:, s]) * (t1[:, s] - a0 * t2[:, s])
     red[2, 0] = row_of([k0, k1, k2, k3])
     near1 = reduction(2, near)
-    start(near1)
 
     add_received(t2, y2, v3)
 
-    arrive(near1)
+    near1.wait_recv()
     red[3, 0] = summed(2, group)
     far1 = reduction(3, far)
-    start(far1)
-    arrive(far1)
+    far1.wait_recv()
     sums = spread_row(summed(3, others))
     k0, k1, k2, k3 = (sums[i * pairs : (i + 1) * pairs] for i in range(4))
 
@@ -362,8 +360,7 @@
         resid[:, s] = r2 - a2 * ap2
 
     for copies in (ex0, ex1, ex2, near0, far0, near1, far1):
-        for copy in copies:
-            copy.wait_send()
+        copies.wait_send()
 
 
 def write_out(volt, resid, volt_out, resid_out, sems):
@@ -411,10 +408,10 @@
             pltpu.VMEM((links, pairs, LANES), F32),
             pltpu.VMEM((links, pairs, LANES), F32),
             pltpu.VMEM((4, most, 1, LANES), F32),
-            pltpu.SemaphoreType.DMA((3, links)),
-            pltpu.SemaphoreType.DMA((3, links)),
-            pltpu.SemaphoreType.DMA((4, most)),
-            pltpu.SemaphoreType.DMA((4, most)),
+            pltpu.SemaphoreType.DMA((3,)),
+            pltpu.SemaphoreType.DMA((3,)),
+            pltpu.SemaphoreType.DMA((4,)),
+            pltpu.SemaphoreType.DMA((4,)),
         ],
         compiler_params=pltpu.CompilerParams(
             collective_id=0, has_side_effects=True, vmem_limit_bytes=48 * 1024 * 1024

time: 38.2 us -> 35.3 us (0.924)
  Pallas kernels: 37.5 us -> 34.5 us
    pallas_call x1, Pallas kernels: 36.7 us -> 33.8 us  [solve(): pl.pallas_call(functools.partial(kernel, parts, group), out_shape=(jax.Sh...]
where the time goes in v3:
time: 35.3 us; the launch traced here: 35.2 us
  Pallas kernels  34.5 us (98%)
  between operations  0.64 us (2%)
    pallas_call x1, Pallas kernels, solve(): pl.pallas_call(functools.partial(kernel, parts, group), out_shape=(jax.Sh...  33.8 us
    pallas_call x1, Pallas kernels, solve(): pl.pallas_call(write_out, out_shape=(jax.ShapeDtypeStruct((pairs, nodes),...  0.72 us

profile of v3, /device:TPU:1, one launch (start us, length us, event | category | flops | bytes accessed | tf_op | source)
XLA Modules:
  0.0 35.2 jit_solution(3734318912053705143)
XLA Ops:
  0.6 33.8 %shard_map.68 = (f32[16,2048]{1,0:T(8,128)S(1)}, f32[16,2048]{1,0:T(8,128)S(1)}) custom-call(f32[16,2048]{1,0:T(8,128)} %cur_in.1, f32[1,2048]{1,0:T(1,128)} %bitcast.2, f32[1,2048]{1,0:T(1,128)} %bitcast.3, s32[9,2048]{1,0:T(8,128)} %ell_in.1, s32[6,128]{1,0:T(8,128)} %send_in.1), custom_call_target="tpu_custom_call" | custom-call | tf_op jit(solution)/shard_map/pallas_call | solution.py:383
  34.4 0.7 %shard_map.69 = (f32[16,2048]{1,0:T(8,128)}, f32[16,2048]{1,0:T(8,128)}) custom-call(f32[16,2048]{1,0:T(8,128)S(1)} %get-tuple-element.4.volt, f32[16,2048]{1,0:T(8,128)S(1)} %get-tuple-element.5.resid), custom_call_target="tpu_custom_call" | custom-call | tf_op jit(solution)/shard_map/pallas_call | solution.py:420

commit v4 on v3

--- a/solution.py
+++ b/solution.py
@@ -8,7 +8,7 @@
 from jax.sharding import PartitionSpec as P
 
 MESH = pl.DeviceIdType.MESH
-F32, BF16, I16, I32 = jnp.float32, jnp.bfloat16, jnp.int16, jnp.int32
+F32, BF16, I32 = jnp.float32, jnp.bfloat16, jnp.int32
 LANES = 128
 WIDE = 256
 DIGITS = 8
@@ -32,7 +32,7 @@
 
 def kernel(
     parts, group, cur_in, cond_in, gnd_in, ell_in, send_in, volt, resid,
-    cur, cond, gnd, ell, send, in_sem, adj, sel, v1, v2, v3, y0, y1, y2, diag, lhs, blhs, slhs, wsend, u0, u1, u2, t0, t1, t2,
+    cur, cond, gnd, ell, send, in_sem, adj, from_slot, v1, v2, v3, y0, y1, y2, diag, lhs, wsend, u0, u1, u2, t0, t1, t2,
     out0, out1, out2, in0, in1, in2, red, ex_send, ex_recv, red_send, red_recv,
 ):
     pairs, nodes = cur.shape
@@ -60,9 +60,6 @@
     near = [mine * group + lax.rem(place + d, group) for d in range(1, group)]
     far = [lax.rem(mine + d, others) * group + place for d in range(1, others)]
 
-    barrier = pltpu.get_barrier_semaphore()
-    for peer in neighbours + near + far:
-        pl.semaphore_signal(barrier, inc=1, device_id={"dom": peer}, device_id_type=MESH)
     loads = [
         pltpu.make_async_copy(source, target, in_sem.at[i])
         for i, (source, target) in enumerate(
@@ -74,46 +71,48 @@
     for i in range(1, 4):
         loads[i].start()
 
-    ones = jnp.ones((16, LANES), BF16)
-    none = jnp.zeros((16, LANES), BF16)
-    row_ids = lax.broadcasted_iota(I32, (16, LANES), 0).astype(I16)
+    barrier = pltpu.get_barrier_semaphore()
+    for peer in neighbours + near + far:
+        pl.semaphore_signal(barrier, inc=1, device_id={"dom": peer}, device_id_type=MESH)
     word_ids = lax.broadcasted_iota(I32, (8, LANES), 0)
     no_word = jnp.zeros((8, LANES), I32)
     words = nodes // DIGITS
 
-    def spread(row):
-        return jnp.broadcast_to(row, (16, LANES)).astype(I16)
-
-    with jax.named_scope("selbuild"):
+    def taken(x, lane):
+        return jnp.take_along_axis(x, lane, axis=1, mode="promise_in_bounds")
+
+    def picked(source, rows):
+        found = []
+        for o in range(links):
+            node = jnp.broadcast_to(send[o : o + 1, :], (8, LANES))
+            lane, tile = node & (LANES - 1), lax.shift_right_arithmetic(node, 7)
+            parts_found = [jnp.zeros((8, LANES), F32)] * (rows // 8)
+            for k, s in enumerate(tiles(nodes)):
+                here = tile == k
+                for i in range(rows // 8):
+                    parts_found[i] = jnp.where(here, taken(source(i, s), lane), parts_found[i])
+            found.append(jnp.concatenate(parts_found, axis=0))
+        return found
+
+    def field_rows(field):
+        return lambda i, s: field[i * 8 : i * 8 + 8, s]
+
+    with jax.named_scope("pick_cur"):
         loads[4].wait()
-        listed = [spread(send[o : o + 1, :]) for o in range(links)]
-        for at in range(0, nodes, 16):
-            ids = row_ids + jnp.int16(at)
-            for o in range(links):
-                sel[o, at : at + 16, :] = jnp.where(listed[o] == ids, ones, none)
-
-    def sel_block(b):
-        return jnp.concatenate([sel[b // LANES], sel[b // LANES + 1]], axis=1)
-
-    def picked(y_parts, rows):
-        for i, piece in enumerate(y_parts):
-            slhs[i * rows : (i + 1) * rows, :] = piece
-
-    loads[0].wait()
-    loads[1].wait()
-    slhs[...] = jnp.zeros_like(slhs)
-    picked(pieces(cur[...]), pairs)
-    for i, piece in enumerate(pieces(cond[...])):
-        slhs[3 * pairs + i : 3 * pairs + i + 1, :] = piece
-    for b in range(0, bound, WIDE):
-        y = jnp.dot(slhs[...], sel_block(b), preferred_element_type=F32)
-        u0[:, b : b + WIDE] = joined(y, 0, pairs)
-        c_part = joined(y, 3 * pairs, 1)
-        wsend[:, b : b + WIDE] = jnp.broadcast_to(c_part, (8, WIDE))
-    for o in range(links):
-        s = slice(o * LANES, (o + 1) * LANES)
-        out0[o, 0:pairs, :] = u0[:, s]
-        out0[o, pairs : pairs + 8, :] = wsend[:, s]
+        loads[0].wait()
+        loads[1].wait()
+        for o, (u, c) in enumerate(
+            zip(
+                picked(field_rows(cur), pairs),
+                picked(lambda i, s: jnp.broadcast_to(cond[:, s], (8, LANES)), 8),
+                strict=True,
+            )
+        ):
+            s = slice(o * LANES, (o + 1) * LANES)
+            u0[:, s] = u
+            wsend[:, s] = c
+            out0[o, 0:pairs, :] = u
+            out0[o, pairs : pairs + 8, :] = c
 
     def exchange(step, out, into):
         for o in range(links):
@@ -157,13 +156,11 @@
                 last = r == DIGITS - 1
                 digit = lax.shift_right_logical(chunk, 4 * r) if last else chunk & (15 << (4 * r))
                 adj[t, r * words + h : r * words + h + 64, :] = digit.astype(F32).astype(BF16)
-        remote = spread(jnp.max(block, axis=0, keepdims=True))
-        for at in range(nodes, nodes + bound, 16):
-            adj[t, at : at + 16, :] = jnp.where(remote == row_ids + jnp.int16(at), ones, none)
+        from_slot[t] = jnp.max(block, axis=0, keepdims=True) - nodes
         return 0
 
-    def adj_block(b, first, last):
-        return jnp.concatenate([adj[b // LANES, first:last, :], adj[b // LANES + 1, first:last, :]], axis=1)
+    def adj_block(b):
+        return jnp.concatenate([adj[b // LANES], adj[b // LANES + 1]], axis=1)
 
     def scale_of(r):
         return 1.0 if r == DIGITS - 1 else 16.0**-r
@@ -192,7 +189,7 @@
         rows = 7 * pairs if first else 6 * pairs
         for b in range(0, nodes, WIDE):
             s = slice(b, b + WIDE)
-            prod = jnp.dot(lhs[0:rows, :], adj_block(b, 0, nodes), preferred_element_type=F32)
+            prod = jnp.dot(lhs[0:rows, :], adj_block(b), preferred_element_type=F32)
             c = cond[:, s]
             if first:
                 extra = prod[6 * pairs :]
@@ -200,21 +197,21 @@
                 diag[:, s] = gnd[:, s] + half * (c * extra[3:4] + around)
             y[:, s] = diag[:, s] * v[:, s] - half * (c * joined(prod, 0, pairs) + joined(prod, 3 * pairs, pairs))
 
-    def pick_listed(y, start_with):
-        picked(pieces(y[...]), pairs)
-        got = []
-        for b in range(0, bound, WIDE):
-            prod = jnp.dot(slhs[0 : 3 * pairs, :], sel_block(b), preferred_element_type=F32)
-            got.append(joined(prod, 0, pairs))
-        return got
-
     def add_received(t, y, v):
-        for i, piece in enumerate(pieces(t[...])):
-            blhs[i * pairs : (i + 1) * pairs, :] = piece
-        for b in range(0, nodes, WIDE):
-            s = slice(b, b + WIDE)
-            prod = jnp.dot(blhs[...], adj_block(b, nodes, nodes + bound), preferred_element_type=F32)
-            v[:, s] = y[:, s] + joined(prod, 0, pairs)
+        for k, s in enumerate(tiles(nodes)):
+            slot = jnp.broadcast_to(from_slot[k], (8, LANES))
+            lane, link = slot & (LANES - 1), lax.shift_right_arithmetic(slot, 7)
+            found = [jnp.zeros((8, LANES), F32)] * (pairs // 8)
+            for o, part in enumerate(tiles(bound)):
+                here = link == o
+                for i in range(pairs // 8):
+                    found[i] = jnp.where(here, taken(t[i * 8 : i * 8 + 8, part], lane), found[i])
+            v[:, s] = y[:, s] + jnp.concatenate(found, axis=0)
+
+    def pass_on(y, u, out):
+        for o, found in enumerate(picked(field_rows(y), pairs)):
+            u[:, o * LANES : (o + 1) * LANES] = found
+            out[o, :, :] = found
 
     def lane_sums(first, second):
         total = None
@@ -261,68 +258,62 @@
         lhs[6 * pairs + 3 : 6 * pairs + 4, s] = jnp.full((1, words), scale_of(r), BF16)
     split_field(cur)
     local_operator(cur, y0, True)
-    m0 = lane_sums(cur, cur)
-    m1 = lane_sums(cur, y0)
-    ys = pick_listed(y0, None)
-
-    def pass_on(u, into, t, ys, u_next, out):
+    pass_on(y0, u1, out1)
+    ex1 = exchange(1, out1, in1)
+
+    red[0, 0] = row_of([lane_sums(cur, cur), lane_sums(cur, y0)])
+    near0 = reduction(0, near)
+
+    def remote_terms(u, other, t):
         for o in range(links):
             s = slice(o * LANES, (o + 1) * LANES)
-            term = wsend[:, s]
-            term = jnp.concatenate([term] * (pairs // 8), axis=0) * (u[:, s] - into[o, 0:pairs, :])
-            t[:, s] = term
-            if u_next is not None:
-                inner = s.start % WIDE
-                nxt = ys[s.start // WIDE][:, inner : inner + LANES] + term
-                u_next[:, s] = nxt
-                out[o, :, :] = nxt
+            weight = jnp.concatenate([wsend[:, s]] * (pairs // 8), axis=0)
+            t[:, s] = weight * (u[:, s] - other(o, s))
 
     ex0.wait_recv()
     for o in range(links):
         s = slice(o * LANES, (o + 1) * LANES)
         live = jnp.broadcast_to(send[o : o + 1, :], (8, LANES)) >= 0
         wsend[:, s] = jnp.where(live, half * (wsend[:, s] + in0[o, pairs : pairs + 8, :]), 0.0)
-    pass_on(u0, in0, t0, ys, u1, out1)
-    ex1 = exchange(1, out1, in1)
-    m1 = m1 + lane_sums(u0, t0)
-    red[0, 0] = row_of([m0, m1])
-    near0 = reduction(0, near)
-
+    remote_terms(u0, lambda o, s: in0[o, 0:pairs, :], t0)
     add_received(t0, y0, v1)
     split_field(v1)
     local_operator(v1, y1, False)
-    ys = pick_listed(y1, None)
-
-    ex1.wait_recv()
-    pass_on(u1, in1, t1, ys, u2, out2)
+    pass_on(y1, u2, out2)
     ex2 = exchange(2, out2, in2)
+
     near0.wait_recv()
     red[1, 0] = summed(0, group)
     far0 = reduction(1, far)
 
+    ex1.wait_recv()
+    u1[...] = u1[...] + t0[...]
+    remote_terms(u1, lambda o, s: in1[o, :, :] - t0[:, s], t1)
     add_received(t1, y1, v2)
     split_field(v2)
     local_operator(v2, y2, False)
 
     ex2.wait_recv()
-    pass_on(u2, in2, t2, None, None, None)
+    u2[...] = u2[...] + t1[...]
+    remote_terms(u2, lambda o, s: in2[o, :, :] - t1[:, s], t2)
     far0.wait_recv()
     first_sums = spread_row(summed(1, others))
-    m0, m1 = first_sums[0:pairs], first_sums[pairs : 2 * pairs]
-    a0 = m0 / m1
+    step = first_sums[0:pairs] / first_sums[pairs : 2 * pairs]
 
     zero = jnp.zeros((pairs, LANES), F32)
-    k0, k1, k2, k3 = zero, zero, zero, zero
+    g0, g1, h0, h1, h2, h3 = zero, zero, zero, zero, zero, zero
     for s in tiles(nodes):
-        r1 = cur[:, s] - a0 * v1[:, s]
-        q1 = v1[:, s] - a0 * v2[:, s]
-        k0 = k0 + r1 * r1
-        k1 = k1 + r1 * q1
-        k2 = k2 + q1 * q1
-        k3 = k3 + q1 * (y1[:, s] - a0 * y2[:, s])
+        w = cur[:, s] - step * v1[:, s]
+        z = v1[:, s] - step * v2[:, s]
+        g0 = g0 + cur[:, s] * cur[:, s]
+        g1 = g1 + cur[:, s] * w
+        h0 = h0 + w * w
+        h1 = h1 + w * z
+        h2 = h2 + z * z
+        h3 = h3 + z * (y1[:, s] - step * y2[:, s])
     for s in tiles(bound):
-        k3 = k3 + (u1[:, s] - a0 * u2[:, s]) * (t1[:, s] - a0 * t2[:, s])
-    red[2, 0] = row_of([k0, k1, k2, k3])
+        h3 = h3 + (u1[:, s] - step * u2[:, s]) * (t1[:, s] - step * t2[:, s])
+    red[2, 0] = row_of([g0, g1, h0, h1, h2, h3])
     near1 = reduction(2, near)
 
     add_received(t2, y2, v3)
@@ -332,7 +323,20 @@
     far1 = reduction(3, far)
     far1.wait_recv()
     sums = spread_row(summed(3, others))
-    k0, k1, k2, k3 = (sums[i * pairs : (i + 1) * pairs] for i in range(4))
+    m0, g1, h0, h1, h2, h3 = (sums[i * pairs : (i + 1) * pairs] for i in range(6))
+
+    tilt = g1 / (m0 - g1)
+    lead = 1.0 + tilt
+    a0 = step * lead
+    rz = (g1 - h0) / step
+    az = (rz - h1) / step
+    aa = (m0 - 2.0 * g1 + h0) / (step * step)
+    aaz = (az - h2) / step
+    aaa = (aa - az) / step
+    k0 = lead * (lead * h0 - tilt * g1)
+    k1 = lead * (lead * h1 - tilt * rz) + tilt * k0 / a0
+    k2 = lead * (lead * h2 - 2.0 * tilt * az) + tilt * tilt * aa
+    k3 = lead * (lead * h3 - 2.0 * tilt * aaz) + tilt * tilt * aaa
 
     b1 = k0 / m0
     a1 = k0 / (k1 - b1 * k0 / a0)
@@ -392,13 +396,11 @@
             pltpu.VMEM(ell_cols.shape, I32),
             pltpu.VMEM(send_rows.shape, I32),
             pltpu.SemaphoreType.DMA((5,)),
-            pltpu.VMEM((nodes // LANES, nodes + bound, LANES), BF16),
-            pltpu.VMEM((links, nodes, LANES), BF16),
+            pltpu.VMEM((nodes // LANES, nodes, LANES), BF16),
+            pltpu.VMEM((nodes // LANES, 1, LANES), I32),
             field, field, field, field, field, field,
             pltpu.VMEM((1, nodes), F32),
             pltpu.VMEM((7 * pairs, nodes), BF16),
-            pltpu.VMEM((3 * pairs, bound), BF16),
-            pltpu.VMEM((4 * pairs, nodes), BF16),
             pltpu.VMEM((8, bound), F32),
             edge, edge, edge, edge, edge, edge,
             pltpu.VMEM((links, pairs + 8, LANES), F32),

time: 35.3 us -> 34.1 us (0.966)
  Pallas kernels: 34.5 us -> 33.4 us
    pallas_call x1, Pallas kernels: 33.8 us -> 32.7 us  [solve(): pl.pallas_call(functools.partial(kernel, parts, group), out_shape=(jax.Sh...]
where the time goes in v4:
time: 34.1 us; the launch traced here: 34 us
  Pallas kernels  33.4 us (98%)
  between operations  0.64 us (2%)
    pallas_call x1, Pallas kernels, solve(): pl.pallas_call(functools.partial(kernel, parts, group), out_shape=(jax.Sh...  32.7 us
    pallas_call x1, Pallas kernels, solve(): pl.pallas_call(write_out, out_shape=(jax.ShapeDtypeStruct((pairs, nodes),...  0.72 us

profile of v4, /device:TPU:1, one launch (start us, length us, event | category | flops | bytes accessed | tf_op | source)
XLA Modules:
  0.0 34.0 jit_solution(8555379015939262618)
XLA Ops:
  0.6 32.7 %shard_map.68 = (f32[16,2048]{1,0:T(8,128)S(1)}, f32[16,2048]{1,0:T(8,128)S(1)}) custom-call(f32[16,2048]{1,0:T(8,128)} %cur_in.1, f32[1,2048]{1,0:T(1,128)} %bitcast.2, f32[1,2048]{1,0:T(1,128)} %bitcast.3, s32[9,2048]{1,0:T(8,128)} %ell_in.1, s32[6,128]{1,0:T(8,128)} %send_in.1), custom_call_target="tpu_custom_call" | custom-call | tf_op jit(solution)/shard_map/pallas_call | solution.py:387
  33.3 0.7 %shard_map.69 = (f32[16,2048]{1,0:T(8,128)}, f32[16,2048]{1,0:T(8,128)}) custom-call(f32[16,2048]{1,0:T(8,128)S(1)} %get-tuple-element.4.volt, f32[16,2048]{1,0:T(8,128)S(1)} %get-tuple-element.5.resid), custom_call_target="tpu_custom_call" | custom-call | tf_op jit(solution)/shard_map/pallas_call | solution.py:422

commit v5 on v4

--- a/solution.py
+++ b/solution.py
@@ -24,6 +24,34 @@
 
 def joined(y, first, rows):
     return (y[first + 2 * rows : first + 3 * rows] + y[first + rows : first + 2 * rows]) + y[first : first + rows]
+
+
+def two_sum(a, b):
+    s = a + b
+    part = s - a
+    return s, (a - (s - part)) + (b - part)
+
+
+def two_product(a, b):
+    p = a * b
+    wide_a, wide_b = a * 4097.0, b * 4097.0
+    a1 = wide_a - (wide_a - a)
+    b1 = wide_b - (wide_b - b)
+    a2, b2 = a - a1, b - b1
+    return p, ((a1 * b1 - p) + a1 * b2 + a2 * b1) + a2 * b2
+
+
+def pair_add(a, b):
+    s, e = two_sum(a[0], b[0])
+    e = e + (a[1] + b[1])
+    high = s + e
+    return high, e - (high - s)
+
+
+def tree(terms, add):
+    while len(terms) > 1:
+        terms = [add(a, b) for a, b in zip(terms[0::2], terms[1::2], strict=True)]
+    return terms[0]
 
 
 def tiles(width):
@@ -60,6 +88,9 @@
     near = [mine * group + lax.rem(place + d, group) for d in range(1, group)]
     far = [lax.rem(mine + d, others) * group + place for d in range(1, others)]
 
+    barrier = pltpu.get_barrier_semaphore()
+    for peer in far + near[group // 2 - 1 :] + near[: group // 2 - 1] + neighbours:
+        pl.semaphore_signal(barrier, inc=1, device_id={"dom": peer}, device_id_type=MESH)
     loads = [
         pltpu.make_async_copy(source, target, in_sem.at[i])
         for i, (source, target) in enumerate(
@@ -71,9 +102,6 @@
     for i in range(1, 4):
         loads[i].start()
 
-    barrier = pltpu.get_barrier_semaphore()
-    for peer in neighbours + near + far:
-        pl.semaphore_signal(barrier, inc=1, device_id={"dom": peer}, device_id_type=MESH)
     word_ids = lax.broadcasted_iota(I32, (8, LANES), 0)
     no_word = jnp.zeros((8, LANES), I32)
     words = nodes // DIGITS
@@ -220,9 +248,17 @@
             total = term if total is None else total + term
         return total
 
-    def row_of(sums):
+    def send_row(sums):
         blocks = jnp.concatenate(sums + [jnp.zeros((LANES - pairs * len(sums), LANES), F32)], axis=0)
-        return jnp.sum(jnp.transpose(blocks), axis=0, keepdims=True)
+        turned = jnp.transpose(blocks)
+        total = tree([two_sum(turned[i : i + 8], turned[i + 8 : i + 16]) for i in range(0, LANES, 16)], pair_add)
+        for shift in (4, 2, 1):
+            total = pair_add(total, tuple(pltpu.roll(x, shift, axis=0) for x in total))
+        put_row(0, total)
+
+    def put_row(stage, total):
+        red[stage, 0, 0:1, :] = total[0][0:1]
+        red[stage, 0, 1:2, :] = total[1][0:1]
 
     def reduction(stage, peers):
         for d, peer in enumerate(peers, start=1):
@@ -241,10 +277,7 @@
         )
 
     def summed(stage, count):
-        terms = [red[stage, d] for d in range(count)]
-        while len(terms) > 1:
-            terms = [a + b for a, b in zip(terms[0::2], terms[1::2], strict=True)]
-        return terms[0]
+        return tree([(red[stage, d, 0:1, :], red[stage, d, 1:2, :]) for d in range(count)], pair_add)
 
     def spread_row(row):
         return jnp.transpose(jnp.broadcast_to(row, (LANES, LANES)))
@@ -261,9 +294,6 @@
     pass_on(y0, u1, out1)
     ex1 = exchange(1, out1, in1)
 
-    red[0, 0] = row_of([lane_sums(cur, cur), lane_sums(cur, y0)])
-    near0 = reduction(0, near)
-
     def remote_terms(u, other, t):
         for o in range(links):
             s = slice(o * LANES, (o + 1) * LANES)
@@ -281,62 +311,47 @@
     local_operator(v1, y1, False)
     pass_on(y1, u2, out2)
     ex2 = exchange(2, out2, in2)
-
-    near0.wait_recv()
-    red[1, 0] = summed(0, group)
-    far0 = reduction(1, far)
+    moments = [lane_sums(cur, cur), lane_sums(cur, v1), lane_sums(v1, v1)]
 
     ex1.wait_recv()
     u1[...] = u1[...] + t0[...]
     remote_terms(u1, lambda o, s: in1[o, :, :] - t0[:, s], t1)
     add_received(t1, y1, v2)
     split_field(v2)
+    moments += [lane_sums(v1, v2), lane_sums(v2, v2)]
     local_operator(v2, y2, False)
 
     ex2.wait_recv()
     u2[...] = u2[...] + t1[...]
     remote_terms(u2, lambda o, s: in2[o, :, :] - t1[:, s], t2)
-    far0.wait_recv()
-    first_sums = spread_row(summed(1, others))
-    step = first_sums[0:pairs] / first_sums[pairs : 2 * pairs]
-
-    zero = jnp.zeros((pairs, LANES), F32)
-    g0, g1, h0, h1, h2, h3 = zero, zero, zero, zero, zero, zero
-    for s in tiles(nodes):
-        w = cur[:, s] - step * v1[:, s]
-        z = v1[:, s] - step * v2[:, s]
-        g0 = g0 + cur[:, s] * cur[:, s]
-        g1 = g1 + cur[:, s] * w
-        h0 = h0 + w * w
-        h1 = h1 + w * z
-        h2 = h2 + z * z
-        h3 = h3 + z * (y1[:, s] - step * y2[:, s])
-    for s in tiles(bound):
-        h3 = h3 + (u1[:, s] - step * u2[:, s]) * (t1[:, s] - step * t2[:, s])
-    red[2, 0] = row_of([g0, g1, h0, h1, h2, h3])
-    near1 = reduction(2, near)
+    moments.append(lane_sums(v2, y2) + lane_sums(u2, t2))
+    send_row(moments)
+    near_sums = reduction(0, near)
 
     add_received(t2, y2, v3)
 
-    near1.wait_recv()
-    red[3, 0] = summed(2, group)
-    far1 = reduction(3, far)
-    far1.wait_recv()
-    sums = spread_row(summed(3, others))
-    m0, g1, h0, h1, h2, h3 = (sums[i * pairs : (i + 1) * pairs] for i in range(6))
-
-    tilt = g1 / (m0 - g1)
-    lead = 1.0 + tilt
-    a0 = step * lead
-    rz = (g1 - h0) / step
-    az = (rz - h1) / step
-    aa = (m0 - 2.0 * g1 + h0) / (step * step)
-    aaz = (az - h2) / step
-    aaa = (aa - az) / step
-    k0 = lead * (lead * h0 - tilt * g1)
-    k1 = lead * (lead * h1 - tilt * rz) + tilt * k0 / a0
-    k2 = lead * (lead * h2 - 2.0 * tilt * az) + tilt * tilt * aa
-    k3 = lead * (lead * h3 - 2.0 * tilt * aaz) + tilt * tilt * aaa
+    near_sums.wait_recv()
+    put_row(1, summed(0, group))
+    far_sums = reduction(1, far)
+    far_sums.wait_recv()
+    high, low = (spread_row(x) for x in summed(1, others))
+    m = [(high[i * pairs : (i + 1) * pairs], low[i * pairs : (i + 1) * pairs]) for i in range(6)]
+
+    m0 = m[0][0]
+    a0 = m0 / m[1][0]
+    square, square_rest = two_product(a0, a0)
+    double = 2.0 * a0
+
+    def shifted(i):
+        p, p_rest = two_product(m[i + 1][0], double)
+        q, q_rest = two_product(m[i + 2][0], square)
+        p_rest = p_rest + m[i + 1][1] * double
+        q_rest = q_rest + (m[i + 2][1] * square + m[i + 2][0] * square_rest)
+        s, s_rest = two_sum(m[i][0], -p)
+        s, t_rest = two_sum(s, q)
+        return s + ((s_rest + t_rest) + (m[i][1] - p_rest + q_rest))
+
+    k0, k1, k2, k3 = (shifted(i) for i in range(4))
 
     b1 = k0 / m0
     a1 = k0 / (k1 - b1 * k0 / a0)
@@ -363,7 +378,7 @@
         volt[:, s] = a0 * w0 + a1 * p1 + a2 * p2
         resid[:, s] = r2 - a2 * ap2
 
-    for copies in (ex0, ex1, ex2, near0, far0, near1, far1):
+    for copies in (ex0, ex1, ex2, near_sums, far_sums):
         copies.wait_send()
 
 
@@ -409,11 +424,11 @@
             pltpu.VMEM((links, pairs + 8, LANES), F32),
             pltpu.VMEM((links, pairs, LANES), F32),
             pltpu.VMEM((links, pairs, LANES), F32),
-            pltpu.VMEM((4, most, 1, LANES), F32),
+            pltpu.VMEM((2, most, 2, LANES), F32),
             pltpu.SemaphoreType.DMA((3,)),
             pltpu.SemaphoreType.DMA((3,)),
-            pltpu.SemaphoreType.DMA((4,)),
-            pltpu.SemaphoreType.DMA((4,)),
+            pltpu.SemaphoreType.DMA((2,)),
+            pltpu.SemaphoreType.DMA((2,)),
         ],
         compiler_params=pltpu.CompilerParams(
             collective_id=0, has_side_effects=True, vmem_limit_bytes=48 * 1024 * 1024

time: 34.1 us -> 31 us (0.909)
  Pallas kernels: 33.4 us -> 30.3 us
    pallas_call x1, Pallas kernels: 32.7 us -> 29.5 us  [solve(): pl.pallas_call(functools.partial(kernel, parts, group), out_shape=(jax.Sh...]
where the time goes in v5:
time: 31 us; the launch traced here: 30.9 us
  Pallas kernels  30.3 us (98%)
  between operations  0.64 us (2%)
    pallas_call x1, Pallas kernels, solve(): pl.pallas_call(functools.partial(kernel, parts, group), out_shape=(jax.Sh...  29.5 us
    pallas_call x1, Pallas kernels, solve(): pl.pallas_call(write_out, out_shape=(jax.ShapeDtypeStruct((pairs, nodes),...  0.72 us

profile of v5, /device:TPU:1, one launch (start us, length us, event | category | flops | bytes accessed | tf_op | source)
XLA Modules:
  0.0 30.9 jit_solution(6738505159812413378)
XLA Ops:
  0.6 29.5 %shard_map.68 = (f32[16,2048]{1,0:T(8,128)S(1)}, f32[16,2048]{1,0:T(8,128)S(1)}) custom-call(f32[16,2048]{1,0:T(8,128)} %cur_in.1, f32[1,2048]{1,0:T(1,128)} %bitcast.2, f32[1,2048]{1,0:T(1,128)} %bitcast.3, s32[9,2048]{1,0:T(8,128)} %ell_in.1, s32[6,128]{1,0:T(8,128)} %send_in.1), custom_call_target="tpu_custom_call" | custom-call | tf_op jit(solution)/shard_map/pallas_call | solution.py:402
  30.2 0.7 %shard_map.69 = (f32[16,2048]{1,0:T(8,128)}, f32[16,2048]{1,0:T(8,128)}) custom-call(f32[16,2048]{1,0:T(8,128)S(1)} %get-tuple-element.4.volt, f32[16,2048]{1,0:T(8,128)S(1)} %get-tuple-element.5.resid), custom_call_target="tpu_custom_call" | custom-call | tf_op jit(solution)/shard_map/pallas_call | solution.py:437

commit v6 on v5

--- a/solution.py
+++ b/solution.py
@@ -74,7 +74,7 @@
     mine, place = me // group, me % group
 
     assert reach == 3
-    neighbours, landing = [], []
+    neighbours, landing, side_of = [], [], []
     for o, e in enumerate(offsets):
         d = abs(e)
         edge = me if e < 0 else parts - 1 - me
@@ -85,12 +85,21 @@
         spare_slot = reach - spare_d if e < 0 else reach - 1 + spare_d
         neighbours.append(jnp.where(inside, me + e, spare_peer))
         landing.append(jnp.where(inside, links - 1 - o, spare_slot))
-    near = [mine * group + lax.rem(place + d, group) for d in range(1, group)]
-    far = [lax.rem(mine + d, others) * group + place for d in range(1, others)]
-
-    barrier = pltpu.get_barrier_semaphore()
-    for peer in far + near[group // 2 - 1 :] + near[: group // 2 - 1] + neighbours:
-        pl.semaphore_signal(barrier, inc=1, device_id={"dom": peer}, device_id_type=MESH)
+        side_of.append(jnp.where(inside, 1 if e < 0 else 0, 0 if e < 0 else 1))
+    def steps(d, count):
+        return min(d, count - d)
+
+    near = [
+        (d, mine * group + lax.rem(place + d, group))
+        for d in sorted(range(1, group), key=lambda d: -steps(d, group))
+    ]
+    side = 4 if others == 16 else 2
+    row, column = mine // side, mine % side
+    far = [
+        (d, (lax.rem(row + d // side, side) * side + lax.rem(column + d % side, side)) * group + place)
+        for d in sorted(range(1, others), key=lambda d: -steps(d // side, side) - steps(d % side, side))
+    ]
+
     loads = [
         pltpu.make_async_copy(source, target, in_sem.at[i])
         for i, (source, target) in enumerate(
@@ -102,6 +111,9 @@
     for i in range(1, 4):
         loads[i].start()
 
+    barrier = pltpu.get_barrier_semaphore()
+    for peer in neighbours + [peer for _, peer in near + far]:
+        pl.semaphore_signal(barrier, inc=1, device_id={"dom": peer}, device_id_type=MESH)
     word_ids = lax.broadcasted_iota(I32, (8, LANES), 0)
     no_word = jnp.zeros((8, LANES), I32)
     words = nodes // DIGITS
@@ -109,11 +121,14 @@
     def taken(x, lane):
         return jnp.take_along_axis(x, lane, axis=1, mode="promise_in_bounds")
 
+    def places(o):
+        node = jnp.broadcast_to(send[o : o + 1, :], (8, LANES))
+        return node & (LANES - 1), lax.shift_right_arithmetic(node, 7)
+
     def picked(source, rows):
         found = []
         for o in range(links):
-            node = jnp.broadcast_to(send[o : o + 1, :], (8, LANES))
-            lane, tile = node & (LANES - 1), lax.shift_right_arithmetic(node, 7)
+            lane, tile = places(o)
             parts_found = [jnp.zeros((8, LANES), F32)] * (rows // 8)
             for k, s in enumerate(tiles(nodes)):
                 here = tile == k
@@ -140,22 +155,25 @@
             u0[:, s] = u
             wsend[:, s] = c
             out0[o, 0:pairs, :] = u
-            out0[o, pairs : pairs + 8, :] = c
+            out0[o, pairs : pairs + 1, :] = c[0:1]
 
     def exchange(step, out, into):
-        for o in range(links):
+        for o in sorted(range(links), key=lambda o: -abs(offsets[o])):
             pltpu.make_async_remote_copy(
                 src_ref=out.at[o],
                 dst_ref=into.at[landing[o]],
                 send_sem=ex_send.at[step],
-                recv_sem=ex_recv.at[step],
+                recv_sem=ex_recv.at[step, side_of[o]],
                 device_id={"dom": neighbours[o]},
                 device_id_type=MESH,
             ).start()
-        return pltpu.make_async_remote_copy(
-            src_ref=out, dst_ref=into, send_sem=ex_send.at[step], recv_sem=ex_recv.at[step],
-            device_id={"dom": neighbours[0]}, device_id_type=MESH,
-        )
+        return [
+            pltpu.make_async_remote_copy(
+                src_ref=out.at[half], dst_ref=into.at[half], send_sem=ex_send.at[step], recv_sem=ex_recv.at[step, i],
+                device_id={"dom": neighbours[0]}, device_id_type=MESH,
+            )
+            for i, half in enumerate((slice(0, reach), slice(reach, links)))
+        ]
 
     def build(t, _):
         off = pl.multiple_of(t * LANES, LANES)
@@ -193,19 +211,17 @@
     def scale_of(r):
         return 1.0 if r == DIGITS - 1 else 16.0**-r
 
-    def split_field(v):
-        for r in range(DIGITS):
-            s = slice(r * words, (r + 1) * words)
-            part = v[:, s] * scale_of(r)
-            for i, piece in enumerate(pieces(part)):
-                lhs[i * pairs : (i + 1) * pairs, s] = piece
-            for i, piece in enumerate(pieces(part * cond[:, s])):
-                lhs[(3 + i) * pairs : (4 + i) * pairs, s] = piece
+    def split_part(value, s):
+        part = value * scale_of(s.start // words)
+        for i, piece in enumerate(pieces(part)):
+            lhs[i * pairs : (i + 1) * pairs, s] = piece
+        for i, piece in enumerate(pieces(part * cond[:, s])):
+            lhs[(3 + i) * pairs : (4 + i) * pairs, s] = piece
 
     half = 0.5
     with jax.named_scope("adj_a"):
         loads[3].wait()
-        ahead = jnp.where(place < group // 2, nodes // LANES, nodes // LANES // 4)
+        ahead = jnp.where(place < group // 2, nodes // LANES, nodes // LANES * 7 // 16)
         lax.fori_loop(0, ahead, build, 0)
     with jax.named_scope("barwait"):
         pl.semaphore_wait(barrier, len(neighbours) + len(near) + len(far))
@@ -213,7 +229,10 @@
     with jax.named_scope("adj_b"):
         lax.fori_loop(ahead, nodes // LANES, build, 0)
 
-    def local_operator(v, y, first):
+    def local_operator(v, y, first, u=None, out=None):
+        if u is not None:
+            listed = [places(o) for o in range(links)]
+            found = [[jnp.zeros((8, LANES), F32)] * (pairs // 8) for _ in range(links)]
         rows = 7 * pairs if first else 6 * pairs
         for b in range(0, nodes, WIDE):
             s = slice(b, b + WIDE)
@@ -223,9 +242,23 @@
                 extra = prod[6 * pairs :]
                 around = joined(extra, 0, 1)
                 diag[:, s] = gnd[:, s] + half * (c * extra[3:4] + around)
-            y[:, s] = diag[:, s] * v[:, s] - half * (c * joined(prod, 0, pairs) + joined(prod, 3 * pairs, pairs))
-
-    def add_received(t, y, v):
+            result = diag[:, s] * v[:, s] - half * (c * joined(prod, 0, pairs) + joined(prod, 3 * pairs, pairs))
+            y[:, s] = result
+            if u is not None:
+                for k in (b // LANES, b // LANES + 1):
+                    inner = k * LANES - b
+                    for o, (lane, tile) in enumerate(listed):
+                        here = tile == k
+                        for i in range(pairs // 8):
+                            piece = result[i * 8 : i * 8 + 8, inner : inner + LANES]
+                            found[o][i] = jnp.where(here, taken(piece, lane), found[o][i])
+        if u is not None:
+            for o in range(links):
+                both = jnp.concatenate(found[o], axis=0)
+                u[:, o * LANES : (o + 1) * LANES] = both
+                out[o, :, :] = both
+
+    def add_received(t, y, v, onward):
         for k, s in enumerate(tiles(nodes)):
             slot = jnp.broadcast_to(from_slot[k], (8, LANES))
             lane, link = slot & (LANES - 1), lax.shift_right_arithmetic(slot, 7)
@@ -234,12 +267,10 @@
                 here = link == o
                 for i in range(pairs // 8):
                     found[i] = jnp.where(here, taken(t[i * 8 : i * 8 + 8, part], lane), found[i])
-            v[:, s] = y[:, s] + jnp.concatenate(found, axis=0)
-
-    def pass_on(y, u, out):
-        for o, found in enumerate(picked(field_rows(y), pairs)):
-            u[:, o * LANES : (o + 1) * LANES] = found
-            out[o, :, :] = found
+            value = y[:, s] + jnp.concatenate(found, axis=0)
+            v[:, s] = value
+            if onward:
+                split_part(value, s)
 
     def lane_sums(first, second):
         total = None
@@ -261,7 +292,7 @@
         red[stage, 0, 1:2, :] = total[1][0:1]
 
     def reduction(stage, peers):
-        for d, peer in enumerate(peers, start=1):
+        for d, peer in peers:
             pltpu.make_async_remote_copy(
                 src_ref=red.at[stage, 0],
                 dst_ref=red.at[stage, d],
@@ -273,7 +304,7 @@
         slots_used = red.at[stage, 1 : len(peers) + 1]
         return pltpu.make_async_remote_copy(
             src_ref=slots_used, dst_ref=slots_used, send_sem=red_send.at[stage], recv_sem=red_recv.at[stage],
-            device_id={"dom": peers[0]}, device_id_type=MESH,
+            device_id={"dom": peers[0][1]}, device_id_type=MESH,
         )
 
     def summed(stage, count):
@@ -289,9 +320,9 @@
         for i, piece in enumerate(pieces(cond[:, s] * scale_of(r))):
             lhs[6 * pairs + i : 6 * pairs + i + 1, s] = piece
         lhs[6 * pairs + 3 : 6 * pairs + 4, s] = jnp.full((1, words), scale_of(r), BF16)
-    split_field(cur)
-    local_operator(cur, y0, True)
-    pass_on(y0, u1, out1)
+    for s in tiles(nodes):
+        split_part(cur[:, s], s)
+    local_operator(cur, y0, True, u1, out1)
     ex1 = exchange(1, out1, in1)
 
     def remote_terms(u, other, t):
@@ -300,35 +331,45 @@
             weight = jnp.concatenate([wsend[:, s]] * (pairs // 8), axis=0)
             t[:, s] = weight * (u[:, s] - other(o, s))
 
-    ex0.wait_recv()
+    ex0[0].wait_recv()
+    ex0[1].wait_recv()
     for o in range(links):
         s = slice(o * LANES, (o + 1) * LANES)
         live = jnp.broadcast_to(send[o : o + 1, :], (8, LANES)) >= 0
-        wsend[:, s] = jnp.where(live, half * (wsend[:, s] + in0[o, pairs : pairs + 8, :]), 0.0)
+        wsend[:, s] = jnp.where(live, half * (wsend[:, s] + in0[o, pairs : pairs + 1, :]), 0.0)
     remote_terms(u0, lambda o, s: in0[o, 0:pairs, :], t0)
-    add_received(t0, y0, v1)
-    split_field(v1)
-    local_operator(v1, y1, False)
-    pass_on(y1, u2, out2)
+    add_received(t0, y0, v1, True)
+    local_operator(v1, y1, False, u2, out2)
     ex2 = exchange(2, out2, in2)
     moments = [lane_sums(cur, cur), lane_sums(cur, v1), lane_sums(v1, v1)]
 
-    ex1.wait_recv()
+    ex1[0].wait_recv()
+    ex1[1].wait_recv()
     u1[...] = u1[...] + t0[...]
     remote_terms(u1, lambda o, s: in1[o, :, :] - t0[:, s], t1)
-    add_received(t1, y1, v2)
-    split_field(v2)
+    add_received(t1, y1, v2, True)
     moments += [lane_sums(v1, v2), lane_sums(v2, v2)]
     local_operator(v2, y2, False)
 
-    ex2.wait_recv()
-    u2[...] = u2[...] + t1[...]
-    remote_terms(u2, lambda o, s: in2[o, :, :] - t1[:, s], t2)
-    moments.append(lane_sums(v2, y2) + lane_sums(u2, t2))
+    def last_terms(side):
+        share = jnp.zeros((pairs, LANES), F32)
+        for o in side:
+            s = slice(o * LANES, (o + 1) * LANES)
+            here = u2[:, s] + t1[:, s]
+            apart = here - (in2[o, :, :] - t1[:, s])
+            term = jnp.concatenate([wsend[:, s]] * (pairs // 8), axis=0) * apart
+            t2[:, s] = term
+            share = share + term * apart
+        return share
+
+    ex2[1].wait_recv()
+    moments.append(lane_sums(v2, y2) + last_terms(range(reach, links)))
     send_row(moments)
     near_sums = reduction(0, near)
 
-    add_received(t2, y2, v3)
+    ex2[0].wait_recv()
+    last_terms(range(reach))
+    add_received(t2, y2, v3, False)
 
     near_sums.wait_recv()
     put_row(1, summed(0, group))
@@ -338,7 +379,7 @@
     m = [(high[i * pairs : (i + 1) * pairs], low[i * pairs : (i + 1) * pairs]) for i in range(6)]
 
     m0 = m[0][0]
-    a0 = m0 / m[1][0]
+    a0, over_a0 = m0 / m[1][0], m[1][0] / m0
     square, square_rest = two_product(a0, a0)
     double = 2.0 * a0
 
@@ -354,15 +395,15 @@
     k0, k1, k2, k3 = (shifted(i) for i in range(4))
 
     b1 = k0 / m0
-    a1 = k0 / (k1 - b1 * k0 / a0)
-    v1q1 = -(k0 / a0 + k1) / a0
+    a1 = k0 / (k1 - b1 * k0 * over_a0)
+    v1q1 = -(k0 * over_a0 + k1) * over_a0
     r2q1 = k1 - a1 * (k2 + b1 * v1q1)
     rr2 = -a1 * r2q1
     b2 = rr2 / k0
-    v1q2 = (v1q1 - k2) / a0
+    v1q2 = (v1q1 - k2) * over_a0
     r2q2 = k2 - a1 * (k3 + b1 * v1q2)
-    r2ar2 = r2q1 - a1 * (r2q2 - b1 * r2q1 / a0)
-    a2 = rr2 / (r2ar2 - b2 * rr2 / a1)
+    r2ar2 = r2q1 - a1 * (r2q2 - b1 * r2q1 * over_a0)
+    a2 = rr2 / (r2ar2 + b2 * r2q1)
 
     for s in tiles(nodes):
         w0, w1, w2, w3 = cur[:, s], v1[:, s], v2[:, s], v3[:, s]
@@ -378,7 +419,7 @@
         volt[:, s] = a0 * w0 + a1 * p1 + a2 * p2
         resid[:, s] = r2 - a2 * ap2
 
-    for copies in (ex0, ex1, ex2, near_sums, far_sums):
+    for copies in (*ex0, *ex1, *ex2, near_sums, far_sums):
         copies.wait_send()
 
 
@@ -418,15 +459,15 @@
             pltpu.VMEM((7 * pairs, nodes), BF16),
             pltpu.VMEM((8, bound), F32),
             edge, edge, edge, edge, edge, edge,
-            pltpu.VMEM((links, pairs + 8, LANES), F32),
+            pltpu.VMEM((links, pairs + 1, LANES), F32),
             pltpu.VMEM((links, pairs, LANES), F32),
             pltpu.VMEM((links, pairs, LANES), F32),
-            pltpu.VMEM((links, pairs + 8, LANES), F32),
+            pltpu.VMEM((links, pairs + 1, LANES), F32),
             pltpu.VMEM((links, pairs, LANES), F32),
             pltpu.VMEM((links, pairs, LANES), F32),
             pltpu.VMEM((2, most, 2, LANES), F32),
             pltpu.SemaphoreType.DMA((3,)),
-            pltpu.SemaphoreType.DMA((3,)),
+            pltpu.SemaphoreType.DMA((3, 2)),
             pltpu.SemaphoreType.DMA((2,)),
             pltpu.SemaphoreType.DMA((2,)),
         ],

time: 31 us -> 31.3 us (level)
    pallas_call x1, Pallas kernels: 29.5 us -> 29.9 us  [solve(): pl.pallas_call(functools.partial(kernel, parts, group), out_shape=(jax.Sh...]
where the time goes in v6:
time: 31.3 us; the launch traced here: 31.2 us
  Pallas kernels  30.6 us (98%)
  between operations  0.64 us (2%)
    pallas_call x1, Pallas kernels, solve(): pl.pallas_call(functools.partial(kernel, parts, group), out_shape=(jax.Sh...  29.9 us
    pallas_call x1, Pallas kernels, solve(): pl.pallas_call(write_out, out_shape=(jax.ShapeDtypeStruct((pairs, nodes),...  0.72 us

profile of v6, /device:TPU:1, one launch (start us, length us, event | category | flops | bytes accessed | tf_op | source)
XLA Modules:
  0.0 31.2 jit_solution(8400957707384850389)
XLA Ops:
  0.6 29.9 %shard_map.68 = (f32[16,2048]{1,0:T(8,128)S(1)}, f32[16,2048]{1,0:T(8,128)S(1)}) custom-call(f32[16,2048]{1,0:T(8,128)} %cur_in.1, f32[1,2048]{1,0:T(1,128)} %bitcast.2, f32[1,2048]{1,0:T(1,128)} %bitcast.3, s32[9,2048]{1,0:T(8,128)} %ell_in.1, s32[6,128]{1,0:T(8,128)} %send_in.1), custom_call_target="tpu_custom_call" | custom-call | tf_op jit(solution)/shard_map/pallas_call | solution.py:443
  30.5 0.7 %shard_map.69 = (f32[16,2048]{1,0:T(8,128)}, f32[16,2048]{1,0:T(8,128)}) custom-call(f32[16,2048]{1,0:T(8,128)S(1)} %get-tuple-element.4.volt, f32[16,2048]{1,0:T(8,128)S(1)} %get-tuple-element.5.resid), custom_call_target="tpu_custom_call" | custom-call | tf_op jit(solution)/shard_map/pallas_call | solution.py:478

commit v7 on v6

--- a/solution.py
+++ b/solution.py
@@ -60,7 +60,7 @@
 
 def kernel(
     parts, group, cur_in, cond_in, gnd_in, ell_in, send_in, volt, resid,
-    cur, cond, gnd, ell, send, in_sem, adj, from_slot, v1, v2, v3, y0, y1, y2, diag, lhs, wsend, u0, u1, u2, t0, t1, t2,
+    cur, cond, gnd, ell, send, in_sem, adj, from_slot, v1, v2, v3, y0, y1, y2, diag, lhs, wsend, mat, tlhs, c_at, d_at, z_at, u0, u1, u2, t0, t1, t2,
     out0, out1, out2, in0, in1, in2, red, ex_send, ex_recv, red_send, red_recv,
 ):
     pairs, nodes = cur.shape
@@ -154,10 +154,11 @@
             s = slice(o * LANES, (o + 1) * LANES)
             u0[:, s] = u
             wsend[:, s] = c
+            c_at[:, s] = c
             out0[o, 0:pairs, :] = u
             out0[o, pairs : pairs + 1, :] = c[0:1]
 
-    def exchange(step, out, into):
+    def send_all(step, out, into):
         for o in sorted(range(links), key=lambda o: -abs(offsets[o])):
             pltpu.make_async_remote_copy(
                 src_ref=out.at[o],
@@ -167,6 +168,8 @@
                 device_id={"dom": neighbours[o]},
                 device_id_type=MESH,
             ).start()
+
+    def exchange(step, out, into):
         return [
             pltpu.make_async_remote_copy(
                 src_ref=out.at[half], dst_ref=into.at[half], send_sem=ex_send.at[step], recv_sem=ex_recv.at[step, i],
@@ -174,6 +177,27 @@
             )
             for i, half in enumerate((slice(0, reach), slice(reach, links)))
         ]
+
+    def fill_counts(into, g, p, count, digits):
+        word = list(p)
+        for i in range(slots):
+            for j in range(i):
+                same = g[i] == g[j]
+                word[i] = word[i] + jnp.where(same, p[j], no_word)
+                word[j] = word[j] + jnp.where(same, p[i], no_word)
+        for h in range(0, count, 64):
+            chunk = []
+            for q in range(h, h + 64, 8):
+                ids = word_ids + q
+                acc = no_word
+                for s in range(slots):
+                    acc = jnp.where(g[s] == ids, word[s], acc)
+                chunk.append(acc)
+            chunk = jnp.concatenate(chunk, axis=0)
+            for r in range(digits):
+                last = r == DIGITS - 1
+                digit = lax.shift_right_logical(chunk, 4 * r) if last else chunk & (15 << (4 * r))
+                into[r * count + h : r * count + h + 64, :] = digit.astype(F32).astype(BF16)
 
     def build(t, _):
         off = pl.multiple_of(t * LANES, LANES)
@@ -183,25 +207,7 @@
         wide_p = jnp.left_shift(jnp.ones_like(block), jnp.where(local, (block // words) * 4, 0))
         g = [jnp.broadcast_to(wide_g[s : s + 1, :], (8, LANES)) for s in range(slots)]
         p = [jnp.broadcast_to(wide_p[s : s + 1, :], (8, LANES)) for s in range(slots)]
-        word = list(p)
-        for i in range(slots):
-            for j in range(i):
-                same = g[i] == g[j]
-                word[i] = word[i] + jnp.where(same, p[j], no_word)
-                word[j] = word[j] + jnp.where(same, p[i], no_word)
-        for h in range(0, words, 64):
-            chunk = []
-            for q in range(h, h + 64, 8):
-                ids = word_ids + q
-                acc = no_word
-                for s in range(slots):
-                    acc = jnp.where(g[s] == ids, word[s], acc)
-                chunk.append(acc)
-            chunk = jnp.concatenate(chunk, axis=0)
-            for r in range(DIGITS):
-                last = r == DIGITS - 1
-                digit = lax.shift_right_logical(chunk, 4 * r) if last else chunk & (15 << (4 * r))
-                adj[t, r * words + h : r * words + h + 64, :] = digit.astype(F32).astype(BF16)
+        fill_counts(adj.at[t], g, p, words, DIGITS)
         from_slot[t] = jnp.max(block, axis=0, keepdims=True) - nodes
         return 0
 
@@ -225,6 +231,7 @@
         lax.fori_loop(0, ahead, build, 0)
     with jax.named_scope("barwait"):
         pl.semaphore_wait(barrier, len(neighbours) + len(near) + len(far))
+    send_all(0, out0, in0)
     ex0 = exchange(0, out0, in0)
     with jax.named_scope("adj_b"):
         lax.fori_loop(ahead, nodes // LANES, build, 0)
@@ -256,7 +263,8 @@
             for o in range(links):
                 both = jnp.concatenate(found[o], axis=0)
                 u[:, o * LANES : (o + 1) * LANES] = both
-                out[o, :, :] = both
+                if out is not None:
+                    out[o, :, :] = both
 
     def add_received(t, y, v, onward):
         for k, s in enumerate(tiles(nodes)):
@@ -323,6 +331,7 @@
     for s in tiles(nodes):
         split_part(cur[:, s], s)
     local_operator(cur, y0, True, u1, out1)
+    send_all(1, out1, in1)
     ex1 = exchange(1, out1, in1)
 
     def remote_terms(u, other, t):
@@ -330,6 +339,40 @@
             s = slice(o * LANES, (o + 1) * LANES)
             weight = jnp.concatenate([wsend[:, s]] * (pairs // 8), axis=0)
             t[:, s] = weight * (u[:, s] - other(o, s))
+
+    early = place < 4
+
+    @pl.when(early)
+    def _():
+        with jax.named_scope("prep"):
+            for o, d in enumerate(picked(lambda i, s: jnp.broadcast_to(diag[:, s], (8, LANES)), 8)):
+                d_at[:, o * LANES : (o + 1) * LANES] = d
+            for s in tiles(nodes):
+                split_part(y0[:, s], s)
+            local_operator(y0, y1, False, z_at)
+            spans = [(0, 8)] + [(i, i + 1) for i in range(8, slots)]
+            for o in range(links):
+                lane, tile = places(o)
+                g, p = [], []
+                for first, end in spans:
+                    near_by = jnp.full((8, LANES), -1, I32)
+                    for k, s in enumerate(tiles(nodes)):
+                        rows = jnp.broadcast_to(ell[first:end, s], (8, LANES))
+                        near_by = jnp.where(tile == k, taken(rows, lane), near_by)
+                    inner = near_by & (LANES - 1)
+                    outer = jnp.where(near_by < nodes, lax.shift_right_arithmetic(near_by, 7), -1)
+                    slot = jnp.full((8, LANES), -1, I32)
+                    for k in range(nodes // LANES):
+                        known = jnp.broadcast_to(from_slot[k], (8, LANES))
+                        slot = jnp.where(outer == k, taken(known, inner), slot)
+                    word = jnp.where(slot >= 0, slot & (LANES - 1), -1)
+                    power = jnp.left_shift(
+                        jnp.ones_like(slot), jnp.where(slot >= 0, lax.shift_right_arithmetic(slot, 7) * 4, 0)
+                    )
+                    for i in range(end - first):
+                        g.append(jnp.broadcast_to(word[i : i + 1], (8, LANES)))
+                        p.append(jnp.broadcast_to(power[i : i + 1], (8, LANES)))
+                fill_counts(mat.at[o], g, p, LANES, links)
 
     ex0[0].wait_recv()
     ex0[1].wait_recv()
@@ -338,8 +381,42 @@
         live = jnp.broadcast_to(send[o : o + 1, :], (8, LANES)) >= 0
         wsend[:, s] = jnp.where(live, half * (wsend[:, s] + in0[o, pairs : pairs + 1, :]), 0.0)
     remote_terms(u0, lambda o, s: in0[o, 0:pairs, :], t0)
+    def both_halves(x):
+        return jnp.concatenate([x] * (pairs // 8), axis=0)
+
+    @pl.when(early)
+    def _():
+        with jax.named_scope("short"):
+            for r, s in enumerate(tiles(bound)):
+                part = t0[:, s] * 16.0**-r
+                for i, piece in enumerate(pieces(part)):
+                    tlhs[i * pairs : (i + 1) * pairs, s] = piece
+                for i, piece in enumerate(pieces(part * both_halves(c_at[:, s]))):
+                    tlhs[(3 + i) * pairs : (4 + i) * pairs, s] = piece
+            for b in range(0, bound, WIDE):
+                counts = jnp.concatenate([mat[b // LANES], mat[b // LANES + 1]], axis=1)
+                prod = jnp.dot(tlhs[...], counts, preferred_element_type=F32)
+                for o in (b // LANES, b // LANES + 1):
+                    s = slice(o * LANES, (o + 1) * LANES)
+                    half_prod = prod[:, o * LANES - b : (o + 1) * LANES - b]
+                    around = both_halves(c_at[:, s]) * joined(half_prod, 0, pairs)
+                    around = around + joined(half_prod, 3 * pairs, pairs)
+                    value = z_at[:, s] + (both_halves(d_at[:, s]) * t0[:, s] - half * around)
+                    u2[:, s] = value
+                    out2[o, :, :] = value
+            send_all(2, out2, in2)
+
     add_received(t0, y0, v1, True)
-    local_operator(v1, y1, False, u2, out2)
+
+    @pl.when(early)
+    def _():
+        local_operator(v1, y1, False)
+
+    @pl.when(jnp.logical_not(early))
+    def _():
+        local_operator(v1, y1, False, u2, out2)
+        send_all(2, out2, in2)
+
     ex2 = exchange(2, out2, in2)
     moments = [lane_sums(cur, cur), lane_sums(cur, v1), lane_sums(v1, v1)]
 
@@ -458,6 +535,11 @@
             pltpu.VMEM((1, nodes), F32),
             pltpu.VMEM((7 * pairs, nodes), BF16),
             pltpu.VMEM((8, bound), F32),
+            pltpu.VMEM((links, bound, LANES), BF16),
+            pltpu.VMEM((6 * pairs, bound), BF16),
+            pltpu.VMEM((8, bound), F32),
+            pltpu.VMEM((8, bound), F32),
+            edge,
             edge, edge, edge, edge, edge, edge,
             pltpu.VMEM((links, pairs + 1, LANES), F32),
             pltpu.VMEM((links, pairs, LANES), F32),

time: 31.3 us -> 30.3 us (0.968)
  Pallas kernels: 30.6 us -> 29.6 us
    pallas_call x1, Pallas kernels: 29.9 us -> 28.9 us  [solve(): pl.pallas_call(functools.partial(kernel, parts, group), out_shape=(jax.Sh...]
where the time goes in v7:
time: 30.3 us; the launch traced here: 30.2 us
  Pallas kernels  29.6 us (98%)
  between operations  0.64 us (2%)
    pallas_call x1, Pallas kernels, solve(): pl.pallas_call(functools.partial(kernel, parts, group), out_shape=(jax.Sh...  28.9 us
    pallas_call x1, Pallas kernels, solve(): pl.pallas_call(write_out, out_shape=(jax.ShapeDtypeStruct((pairs, nodes),...  0.72 us

profile of v7, /device:TPU:1, one launch (start us, length us, event | category | flops | bytes accessed | tf_op | source)
XLA Modules:
  0.0 30.2 jit_solution(10121191010248873132)
XLA Ops:
  0.6 28.9 %shard_map.68 = (f32[16,2048]{1,0:T(8,128)S(1)}, f32[16,2048]{1,0:T(8,128)S(1)}) custom-call(f32[16,2048]{1,0:T(8,128)} %cur_in.1, f32[1,2048]{1,0:T(1,128)} %bitcast.2, f32[1,2048]{1,0:T(1,128)} %bitcast.3, s32[9,2048]{1,0:T(8,128)} %ell_in.1, s32[6,128]{1,0:T(8,128)} %send_in.1), custom_call_target="tpu_custom_call" | custom-call | tf_op jit(solution)/shard_map/pallas_call | solution.py:520
  29.5 0.7 %shard_map.69 = (f32[16,2048]{1,0:T(8,128)}, f32[16,2048]{1,0:T(8,128)}) custom-call(f32[16,2048]{1,0:T(8,128)S(1)} %get-tuple-element.4.volt, f32[16,2048]{1,0:T(8,128)S(1)} %get-tuple-element.5.resid), custom_call_target="tpu_custom_call" | custom-call | tf_op jit(solution)/shard_map/pallas_call | solution.py:560

commit v8 on v7

--- a/solution.py
+++ b/solution.py
@@ -227,7 +227,8 @@
     half = 0.5
     with jax.named_scope("adj_a"):
         loads[3].wait()
-        ahead = jnp.where(place < group // 2, nodes // LANES, nodes // LANES * 7 // 16)
+        part_of = jnp.where(row == 0, 16, jnp.where(row == 1, 10, 4))
+        ahead = jnp.where(place < group // 2, nodes // LANES, nodes // LANES * part_of // 16)
         lax.fori_loop(0, ahead, build, 0)
     with jax.named_scope("barwait"):
         pl.semaphore_wait(barrier, len(neighbours) + len(near) + len(far))
@@ -448,9 +449,12 @@
     last_terms(range(reach))
     add_received(t2, y2, v3, False)
 
+    for copies in (*ex0, *ex1, *ex2):
+        copies.wait_send()
     near_sums.wait_recv()
     put_row(1, summed(0, group))
     far_sums = reduction(1, far)
+    near_sums.wait_send()
     far_sums.wait_recv()
     high, low = (spread_row(x) for x in summed(1, others))
     m = [(high[i * pairs : (i + 1) * pairs], low[i * pairs : (i + 1) * pairs]) for i in range(6)]
@@ -496,8 +500,7 @@
         volt[:, s] = a0 * w0 + a1 * p1 + a2 * p2
         resid[:, s] = r2 - a2 * ap2
 
-    for copies in (*ex0, *ex1, *ex2, near_sums, far_sums):
-        copies.wait_send()
+    far_sums.wait_send()
 
 
 def write_out(volt, resid, volt_out, resid_out, sems):

time: 30.3 us -> 30.3 us (level)
  no operation moved by 1% of the time
where the time goes in v8:
time: 30.3 us; the launch traced here: 30.2 us
  Pallas kernels  29.6 us (98%)
  between operations  0.64 us (2%)
    pallas_call x1, Pallas kernels, solve(): pl.pallas_call(functools.partial(kernel, parts, group), out_shape=(jax.Sh...  28.9 us
    pallas_call x1, Pallas kernels, solve(): pl.pallas_call(write_out, out_shape=(jax.ShapeDtypeStruct((pairs, nodes),...  0.72 us

profile of v8, /device:TPU:1, one launch (start us, length us, event | category | flops | bytes accessed | tf_op | source)
XLA Modules:
  0.0 30.2 jit_solution(8924001653946295103)
XLA Ops:
  0.6 28.9 %shard_map.68 = (f32[16,2048]{1,0:T(8,128)S(1)}, f32[16,2048]{1,0:T(8,128)S(1)}) custom-call(f32[16,2048]{1,0:T(8,128)} %cur_in.1, f32[1,2048]{1,0:T(1,128)} %bitcast.2, f32[1,2048]{1,0:T(1,128)} %bitcast.3, s32[9,2048]{1,0:T(8,128)} %ell_in.1, s32[6,128]{1,0:T(8,128)} %send_in.1), custom_call_target="tpu_custom_call" | custom-call | tf_op jit(solution)/shard_map/pallas_call | solution.py:523
  29.5 0.7 %shard_map.69 = (f32[16,2048]{1,0:T(8,128)}, f32[16,2048]{1,0:T(8,128)}) custom-call(f32[16,2048]{1,0:T(8,128)S(1)} %get-tuple-element.4.volt, f32[16,2048]{1,0:T(8,128)S(1)} %get-tuple-element.5.resid), custom_call_target="tpu_custom_call" | custom-call | tf_op jit(solution)/shard_map/pallas_call | solution.py:563

commit v9 on v8

--- a/solution.py
+++ b/solution.py
@@ -486,19 +486,15 @@
     r2ar2 = r2q1 - a1 * (r2q2 - b1 * r2q1 * over_a0)
     a2 = rr2 / (r2ar2 + b2 * r2q1)
 
+    wide = 1.0 + b1
+    slope = a0 + a1 * wide
+    c0 = slope + a2 * (1.0 + b2 * wide)
+    c1 = -(a1 * a0) - a2 * (slope + b2 * a0)
+    c2 = a2 * (a1 * a0)
     for s in tiles(nodes):
         w0, w1, w2, w3 = cur[:, s], v1[:, s], v2[:, s], v3[:, s]
-        r1 = w0 - a0 * w1
-        q1 = w1 - a0 * w2
-        q2 = w2 - a0 * w3
-        p1 = r1 + b1 * w0
-        ap1 = q1 + b1 * w1
-        r2 = r1 - a1 * ap1
-        ar2 = q1 - a1 * (q2 + b1 * w2)
-        p2 = r2 + b2 * p1
-        ap2 = ar2 + b2 * ap1
-        volt[:, s] = a0 * w0 + a1 * p1 + a2 * p2
-        resid[:, s] = r2 - a2 * ap2
+        volt[:, s] = c0 * w0 + c1 * w1 + c2 * w2
+        resid[:, s] = w0 - (c0 * w1 + c1 * w2 + c2 * w3)
 
     far_sums.wait_send()
 

time: 30.3 us -> 30.3 us (level)
  no operation moved by 1% of the time
where the time goes in v9:
time: 30.3 us; the launch traced here: 30.2 us
  Pallas kernels  29.5 us (97%)
  between operations  0.64 us (2%)
    pallas_call x1, Pallas kernels, solve(): pl.pallas_call(functools.partial(kernel, parts, group), out_shape=(jax.Sh...  28.8 us
    pallas_call x1, Pallas kernels, solve(): pl.pallas_call(write_out, out_shape=(jax.ShapeDtypeStruct((pairs, nodes),...  0.72 us

profile of v9, /device:TPU:1, one launch (start us, length us, event | category | flops | bytes accessed | tf_op | source)
XLA Modules:
  0.0 30.2 jit_solution(14243138701535527485)
XLA Ops:
  0.6 28.8 %shard_map.68 = (f32[16,2048]{1,0:T(8,128)S(1)}, f32[16,2048]{1,0:T(8,128)S(1)}) custom-call(f32[16,2048]{1,0:T(8,128)} %cur_in.1, f32[1,2048]{1,0:T(1,128)} %bitcast.2, f32[1,2048]{1,0:T(1,128)} %bitcast.3, s32[9,2048]{1,0:T(8,128)} %ell_in.1, s32[6,128]{1,0:T(8,128)} %send_in.1), custom_call_target="tpu_custom_call" | custom-call | tf_op jit(solution)/shard_map/pallas_call | solution.py:519
  29.4 0.7 %shard_map.69 = (f32[16,2048]{1,0:T(8,128)}, f32[16,2048]{1,0:T(8,128)}) custom-call(f32[16,2048]{1,0:T(8,128)S(1)} %get-tuple-element.4.volt, f32[16,2048]{1,0:T(8,128)S(1)} %get-tuple-element.5.resid), custom_call_target="tpu_custom_call" | custom-call | tf_op jit(solution)/shard_map/pallas_call | solution.py:559
